TPU v7x, 512 devices: a 4x2x32 block of a 4x8x32 slice. The times are simulated.
512 devices in a mesh: groups: 2 (over y), shot: 32 (over z), slab: 8 (over x, core).
Axes of the slice: x: 4, y: 2, z: 32, core: 2. Of those that a mesh axis runs over, the one named last changes fastest.
The devices are a block of a 4x8x32 slice.
Arguments:
- model: float32 [128, 64, 128], P(('groups', 'slab')), parts along dimension 0, may hold values from 0.05 to 0.3
- fwd_now: float32 [64, 64, 64, 128], P(('groups', 'shot'), 'slab'), parts along dimension 0, may hold values from -6 to 6
- fwd_next: float32 [64, 64, 64, 128], P(('groups', 'shot'), 'slab'), parts along dimension 0, may hold values from -6 to 6
- adj_now: float32 [64, 64, 64, 128], P(('groups', 'shot'), 'slab'), parts along dimension 0, may hold values from -6 to 6
- adj_next: float32 [64, 64, 64, 128], P(('groups', 'shot'), 'slab'), parts along dimension 0, may hold values from -6 to 6
- wavelet: float32 [64, 8], P(('groups', 'shot')), parts along dimension 0, may hold values from -16 to 16
- misfit: float32 [64, 8, 128], P(('groups', 'shot')), parts along dimension 0, may hold values from -6 to 6
- src_index: int32 [64], P(('groups', 'shot')), parts along dimension 0, may hold values from 0 to 524287
- rec_index: int32 [64, 128], P(('groups', 'shot')), parts along dimension 0, may hold values from 0 to 524287
Outputs:
- new_model: float32 [128, 64, 128], P(('groups', 'slab')), parts along dimension 0
- stepped: float32 [64, 64, 64, 128], P(('groups', 'shot'), 'slab'), parts along dimension 0
- adjoint_start: float32 [64, 64, 64, 128], P(('groups', 'shot'), 'slab'), parts along dimension 0
There are 2 independent parts, one for each index of `groups`. A program takes and returns all parts, laid end to end along the dimension named above; each array names one. Nothing has to cross between parts.
All inputs are finite; a program needn't handle non-finite values. Where the computation divides by a largest or mean magnitude, that divisor is 1e-20 or more.
Results may differ from a plain program's by a relative error of at most 0.00002.
Values sent between devices are 32-bit elements; how exact they have to be, the bound alone decides.
A program may use at most 64 MiB of HBM per device.

v0:
```python
import jax
import jax.numpy as jnp
from jax import lax
from jax.sharding import PartitionSpec as P

ITERS = 8


def extended(block, sides, width):
    for axis, dim in sides:
        count = lax.axis_size(axis)
        forward = [(i, i + 1) for i in range(count - 1)]
        backward = [(target, source) for source, target in forward]
        low = lax.ppermute(
            lax.slice_in_dim(block, block.shape[dim] - width, None, axis=dim), axis, forward
        )
        high = lax.ppermute(lax.slice_in_dim(block, 0, width, axis=dim), axis, backward)
        block = jnp.concatenate([low, block, high], axis=dim)
    return block


def total_of_pieces(value, axis):
    return lax.all_gather(value, axis).sum(0)


def sent_to_all(value, axis):
    devices = lax.axis_size(axis)
    return lax.all_to_all(
        jnp.broadcast_to(value[None], (devices, *value.shape)), axis, 0, 0, tiled=True
    )


def over_copies(value, axis):
    return sent_to_all(value, axis).max(axis=0)


def local_laplace(padded):
    full = jnp.pad(padded, ((0, 0), (0, 0), (1, 1), (1, 1)))
    center = full[:, 1:-1, 1:-1, 1:-1]
    beside = full[:, 2:, 1:-1, 1:-1] + full[:, :-2, 1:-1, 1:-1]
    beside = beside + full[:, 1:-1, 2:, 1:-1] + full[:, 1:-1, :-2, 1:-1]
    beside = beside + full[:, 1:-1, 1:-1, 2:] + full[:, 1:-1, 1:-1, :-2]
    return beside - 6.0 * center


def inject(field, index, values, offset):
    shots = field.shape[0]
    cells = field.shape[1] * field.shape[2] * field.shape[3]
    flat = field.reshape(shots, -1)
    local = index - offset
    valid = (local >= 0) & (local < cells)
    local = jnp.clip(local, 0, cells - 1)
    rows = jnp.arange(shots, dtype=jnp.int32).reshape((shots,) + (1,) * (index.ndim - 1))
    rows = jnp.broadcast_to(rows, index.shape)
    flat = flat.at[rows, local].add(jnp.where(valid, values, 0.0))
    return flat.reshape(field.shape)


def update(model, gradient, peak):
    return jnp.clip(model - 0.1 * gradient / (peak + 1e-06), 0.05, 0.3)


def per_device(model, fwd_now, fwd_next, adj_now, adj_next, wavelet, misfit, src_index, rec_index):
    shots = fwd_now.shape[0]
    depth, width, length = model.shape
    offset = lax.axis_index("slab") * (depth * width * length)
    wave, wave_later = (fwd_now, fwd_next)
    adjoint, adjoint_later = (adj_now, adj_next)
    image = jnp.zeros_like(fwd_now)
    for step in range(ITERS):
        stacked = jnp.concatenate([wave, adjoint], axis=0)
        padded = extended(stacked, (("slab", 1),), 1)
        laps = local_laplace(padded)
        lap_wave = laps[:shots]
        lap_adjoint = laps[shots:]
        image = image + adjoint * lap_wave
        wave_prior = 2.0 * wave - wave_later + model[None] * lap_wave
        wave_prior = inject(wave_prior, src_index, wavelet[:, step], offset)
        adjoint_prior = 2.0 * adjoint - adjoint_later + model[None] * lap_adjoint
        adjoint_prior = inject(adjoint_prior, rec_index, misfit[:, step, :], offset)
        wave_later, wave = (wave, wave_prior)
        adjoint_later, adjoint = (adjoint, adjoint_prior)
    local_image = jnp.sum(image, axis=0)
    gradient = total_of_pieces(local_image, "shot")
    peak = over_copies(jnp.max(jnp.abs(gradient)), "slab")
    new_model = update(model, gradient, peak)
    padded_wave = extended(wave, (("slab", 1),), 1)
    stepped = 2.0 * wave - wave_later + new_model[None] * local_laplace(padded_wave)
    return (new_model, stepped, adjoint)


def solution(mesh):
    in_specs = (
        P(("groups", "slab"), None, None),
        P(("groups", "shot"), "slab", None, None),
        P(("groups", "shot"), "slab", None, None),
        P(("groups", "shot"), "slab", None, None),
        P(("groups", "shot"), "slab", None, None),
        P(("groups", "shot"), None),
        P(("groups", "shot"), None, None),
        P(("groups", "shot")),
        P(("groups", "shot"), None),
    )
    out_specs = (
        P(("groups", "slab"), None, None),
        P(("groups", "shot"), "slab", None, None),
        P(("groups", "shot"), "slab", None, None),
    )
    return jax.shard_map(
        per_device, mesh=mesh, in_specs=in_specs, out_specs=out_specs, check_vma=False
    )
```

profile of v0, /device:TPU:33, one launch (start us, length us, event | category | flops | bytes accessed | tf_op | source)
XLA Modules:
  0.0 316.7 jit_solution(1243490292641437846)
XLA Ops:
  9.2 4.6 %collective-permute-start.1 = (f32[2,1,64,128]{3,2,1,0:T(8,128)S(1)}, f32[2,1,64,128]{3,2,1,0:T(8,128)S(1)}, u32[]{:S(2)}, u32[]{:S(2)}) collective-permute-start(f32[2,1,64,128]{3,2,1,0:T(8,128)S(1)} %get-tuple-element.133), channel_id=1, source_target_pairs={{0,1},{1,2},{2,3},{3,4},{4,5},{5,6},{6,7},{8,9},{9,10},{10,11},{11... | collective-permute-start | bytes 196616 | tf_op jit(solution)/shard_map/ppermute | solution.py:14
  13.8 40.1 %collective-permute-start = (f32[2,1,64,128]{3,2,1,0:T(8,128)S(1)}, f32[2,1,64,128]{3,2,1,0:T(8,128)S(1)}, u32[]{:S(2)}, u32[]{:S(2)}) collective-permute-start(f32[2,1,64,128]{3,2,1,0:T(8,128)S(1)} %get-tuple-element.134), channel_id=1, source_target_pairs={{1,0},{2,1},{3,2},{4,3},{5,4},{6,5},{7,6},{9,8},{10,9},{11,10},{12... | collective-permute-start | bytes 196616 | tf_op jit(solution)/shard_map/ppermute | solution.py:17
  56.9 1.6 fusion.75
  64.5 1.4 scatter_fusion
  65.9 2.0 collective-permute-start.3
  67.9 2.4 collective-permute-start.2
  70.9 2.6 collective-permute-done.2
  78.7 2.0 collective-permute-start.5
  80.7 2.4 collective-permute-start.4
  83.8 2.5 collective-permute-done.4
  91.6 2.0 collective-permute-start.7
  93.5 2.4 collective-permute-start.6
  96.6 2.5 collective-permute-done.6
  104.5 2.0 collective-permute-start.9
  106.4 2.4 collective-permute-start.8
  109.6 2.5 collective-permute-done.8
  115.9 1.6 scatter_fusion.4
  117.5 2.0 collective-permute-start.11
  119.5 2.4 collective-permute-start.10
  122.6 2.5 collective-permute-done.10
  130.4 2.0 collective-permute-start.13
  132.4 2.4 collective-permute-start.12
  135.5 2.5 collective-permute-done.12
  143.1 2.0 collective-permute-start.15
  145.1 2.4 collective-permute-start.14
  147.6 3.2 collective-permute-done.14
  158.5 1.9 collective-permute-start.17
  160.5 2.4 collective-permute-start.16
  162.9 1.4 scatter_fusion.7
  166.0 107.3 %all-gather.2.cloned.1.call-done = f32[32,8,64,128]{3,2,1,0:T(8,128)} async-done(((f32[1,8,64,128]{3,2,1,0:T(8,128)}), f32[32,8,64,128]{3,2,1,0:T(8,128)}) %all-gather.2.cloned.1.call-update) | async-done | bytes 8388624 | tf_op jit(solution)/shard_map/all_gather | solution.py:23
  273.2 4.0 %reduce_sum.8 = f32[8,64,128]{2,1,0:T(8,128)S(1)} reduce(f32[32,8,64,128]{3,2,1,0:T(8,128)} %all-gather.2.cloned.1.call-done, f32[]{:T(128)} %constant.189.clone.1), dimensions={0}, to_apply=%region_8.9 | reduce | flops 2031616 | bytes 8650756 | tf_op jit(solution)/shard_map/reduce_sum | solution.py:23
  278.5 29.0 %all_to_all.6 = f32[8,1,1]{2,1,0:T(1,128)S(1)} all-to-all(f32[8,1,1]{2,1,0:T(1,128)S(1)} %broadcast_in_dim.31), channel_id=1, replica_groups=mesh['groups'=2,'shot'=32,'slab'=8] {'slab'}, dimensions={0} | all-to-all | bytes 64 | tf_op jit(solution)/shard_map/all_to_all | solution.py:28
  (123 shorter events, 35.8 us)
Async XLA Ops:
  7.2 266.1 %all-gather.2.cloned.1.call-start = ((), (), s32[]{:S(2)}) async-start(), calls=%async_computation.1 | async-start | bytes 8650752 | tf_op jit(solution)/shard_map/all_gather | solution.py:23
  9.2 50.7 %collective-permute-start.1 = (f32[2,1,64,128]{3,2,1,0:T(8,128)S(1)}, f32[2,1,64,128]{3,2,1,0:T(8,128)S(1)}, u32[]{:S(2)}, u32[]{:S(2)}) collective-permute-start(f32[2,1,64,128]{3,2,1,0:T(8,128)S(1)} %get-tuple-element.133), channel_id=1, source_target_pairs={{0,1},{1,2},{2,3},{3,4},{4,5},{5,6},{6,7},{8,9},{9,10},{10,11},{11... | collective-permute-start | bytes 196616 | tf_op jit(solution)/shard_map/ppermute | solution.py:14
  13.8 46.1 %collective-permute-start = (f32[2,1,64,128]{3,2,1,0:T(8,128)S(1)}, f32[2,1,64,128]{3,2,1,0:T(8,128)S(1)}, u32[]{:S(2)}, u32[]{:S(2)}) collective-permute-start(f32[2,1,64,128]{3,2,1,0:T(8,128)S(1)} %get-tuple-element.134), channel_id=1, source_target_pairs={{1,0},{2,1},{3,2},{4,3},{5,4},{6,5},{7,6},{9,8},{10,9},{11,10},{12... | collective-permute-start | bytes 196616 | tf_op jit(solution)/shard_map/ppermute | solution.py:17
  60.4 1.0 copy-start.1
  60.4 1.1 copy-start.17
  60.4 1.2 copy-start.19
  60.4 1.2 copy-start.20
  65.9 5.0 %collective-permute-start.3 = (f32[2,1,64,128]{3,2,1,0:T(8,128)S(1)}, f32[2,1,64,128]{3,2,1,0:T(8,128)S(1)}, u32[]{:S(2)}, u32[]{:S(2)}) collective-permute-start(f32[2,1,64,128]{3,2,1,0:T(8,128)S(1)} %get-tuple-element.131), channel_id=1, source_target_pairs={{0,1},{1,2},{2,3},{3,4},{4,5},{5,6},{6,7},{8,9},{9,10},{10,11},{11... | collective-permute-start | bytes 196616 | tf_op jit(solution)/shard_map/ppermute | solution.py:14
  67.9 5.6 %collective-permute-start.2 = (f32[2,1,64,128]{3,2,1,0:T(8,128)S(1)}, f32[2,1,64,128]{3,2,1,0:T(8,128)S(1)}, u32[]{:S(2)}, u32[]{:S(2)}) collective-permute-start(f32[2,1,64,128]{3,2,1,0:T(8,128)S(1)} %get-tuple-element.132), channel_id=1, source_target_pairs={{1,0},{2,1},{3,2},{4,3},{5,4},{6,5},{7,6},{9,8},{10,9},{11,10},{12... | collective-permute-start | bytes 196616 | tf_op jit(solution)/shard_map/ppermute | solution.py:17
  78.7 5.0 %collective-permute-start.5 = (f32[2,1,64,128]{3,2,1,0:T(8,128)S(1)}, f32[2,1,64,128]{3,2,1,0:T(8,128)S(1)}, u32[]{:S(2)}, u32[]{:S(2)}) collective-permute-start(f32[2,1,64,128]{3,2,1,0:T(8,128)S(1)} %get-tuple-element.129), channel_id=1, source_target_pairs={{0,1},{1,2},{2,3},{3,4},{4,5},{5,6},{6,7},{8,9},{9,10},{10,11},{11... | collective-permute-start | bytes 196616 | tf_op jit(solution)/shard_map/ppermute | solution.py:14
  80.7 5.6 %collective-permute-start.4 = (f32[2,1,64,128]{3,2,1,0:T(8,128)S(1)}, f32[2,1,64,128]{3,2,1,0:T(8,128)S(1)}, u32[]{:S(2)}, u32[]{:S(2)}) collective-permute-start(f32[2,1,64,128]{3,2,1,0:T(8,128)S(1)} %get-tuple-element.130), channel_id=1, source_target_pairs={{1,0},{2,1},{3,2},{4,3},{5,4},{6,5},{7,6},{9,8},{10,9},{11,10},{12... | collective-permute-start | bytes 196616 | tf_op jit(solution)/shard_map/ppermute | solution.py:17
  91.6 5.0 %collective-permute-start.7 = (f32[2,1,64,128]{3,2,1,0:T(8,128)S(1)}, f32[2,1,64,128]{3,2,1,0:T(8,128)S(1)}, u32[]{:S(2)}, u32[]{:S(2)}) collective-permute-start(f32[2,1,64,128]{3,2,1,0:T(8,128)S(1)} %get-tuple-element.127), channel_id=1, source_target_pairs={{0,1},{1,2},{2,3},{3,4},{4,5},{5,6},{6,7},{8,9},{9,10},{10,11},{11... | collective-permute-start | bytes 196616 | tf_op jit(solution)/shard_map/ppermute | solution.py:14
  93.5 5.6 %collective-permute-start.6 = (f32[2,1,64,128]{3,2,1,0:T(8,128)S(1)}, f32[2,1,64,128]{3,2,1,0:T(8,128)S(1)}, u32[]{:S(2)}, u32[]{:S(2)}) collective-permute-start(f32[2,1,64,128]{3,2,1,0:T(8,128)S(1)} %get-tuple-element.128), channel_id=1, source_target_pairs={{1,0},{2,1},{3,2},{4,3},{5,4},{6,5},{7,6},{9,8},{10,9},{11,10},{12... | collective-permute-start | bytes 196616 | tf_op jit(solution)/shard_map/ppermute | solution.py:17
  104.5 5.1 %collective-permute-start.9 = (f32[2,1,64,128]{3,2,1,0:T(8,128)S(1)}, f32[2,1,64,128]{3,2,1,0:T(8,128)S(1)}, u32[]{:S(2)}, u32[]{:S(2)}) collective-permute-start(f32[2,1,64,128]{3,2,1,0:T(8,128)S(1)} %get-tuple-element.125), channel_id=1, source_target_pairs={{0,1},{1,2},{2,3},{3,4},{4,5},{5,6},{6,7},{8,9},{9,10},{10,11},{11... | collective-permute-start | bytes 196616 | tf_op jit(solution)/shard_map/ppermute | solution.py:14
  106.4 5.6 %collective-permute-start.8 = (f32[2,1,64,128]{3,2,1,0:T(8,128)S(1)}, f32[2,1,64,128]{3,2,1,0:T(8,128)S(1)}, u32[]{:S(2)}, u32[]{:S(2)}) collective-permute-start(f32[2,1,64,128]{3,2,1,0:T(8,128)S(1)} %get-tuple-element.126), channel_id=1, source_target_pairs={{1,0},{2,1},{3,2},{4,3},{5,4},{6,5},{7,6},{9,8},{10,9},{11,10},{12... | collective-permute-start | bytes 196616 | tf_op jit(solution)/shard_map/ppermute | solution.py:17
  117.5 5.1 %collective-permute-start.11 = (f32[2,1,64,128]{3,2,1,0:T(8,128)S(1)}, f32[2,1,64,128]{3,2,1,0:T(8,128)S(1)}, u32[]{:S(2)}, u32[]{:S(2)}) collective-permute-start(f32[2,1,64,128]{3,2,1,0:T(8,128)S(1)} %get-tuple-element.123), channel_id=1, source_target_pairs={{0,1},{1,2},{2,3},{3,4},{4,5},{5,6},{6,7},{8,9},{9,10},{10,11},{11... | collective-permute-start | bytes 196616 | tf_op jit(solution)/shard_map/ppermute | solution.py:14
  119.5 5.6 %collective-permute-start.10 = (f32[2,1,64,128]{3,2,1,0:T(8,128)S(1)}, f32[2,1,64,128]{3,2,1,0:T(8,128)S(1)}, u32[]{:S(2)}, u32[]{:S(2)}) collective-permute-start(f32[2,1,64,128]{3,2,1,0:T(8,128)S(1)} %get-tuple-element.124), channel_id=1, source_target_pairs={{1,0},{2,1},{3,2},{4,3},{5,4},{6,5},{7,6},{9,8},{10,9},{11,10},{12... | collective-permute-start | bytes 196616 | tf_op jit(solution)/shard_map/ppermute | solution.py:17
  130.4 5.0 %collective-permute-start.13 = (f32[2,1,64,128]{3,2,1,0:T(8,128)S(1)}, f32[2,1,64,128]{3,2,1,0:T(8,128)S(1)}, u32[]{:S(2)}, u32[]{:S(2)}) collective-permute-start(f32[2,1,64,128]{3,2,1,0:T(8,128)S(1)} %get-tuple-element.121), channel_id=1, source_target_pairs={{0,1},{1,2},{2,3},{3,4},{4,5},{5,6},{6,7},{8,9},{9,10},{10,11},{11... | collective-permute-start | bytes 196616 | tf_op jit(solution)/shard_map/ppermute | solution.py:14
  132.4 5.6 %collective-permute-start.12 = (f32[2,1,64,128]{3,2,1,0:T(8,128)S(1)}, f32[2,1,64,128]{3,2,1,0:T(8,128)S(1)}, u32[]{:S(2)}, u32[]{:S(2)}) collective-permute-start(f32[2,1,64,128]{3,2,1,0:T(8,128)S(1)} %get-tuple-element.122), channel_id=1, source_target_pairs={{1,0},{2,1},{3,2},{4,3},{5,4},{6,5},{7,6},{9,8},{10,9},{11,10},{12... | collective-permute-start | bytes 196616 | tf_op jit(solution)/shard_map/ppermute | solution.py:17
  143.1 4.4 %collective-permute-start.15 = (f32[2,1,64,128]{3,2,1,0:T(8,128)S(1)}, f32[2,1,64,128]{3,2,1,0:T(8,128)S(1)}, u32[]{:S(2)}, u32[]{:S(2)}) collective-permute-start(f32[2,1,64,128]{3,2,1,0:T(8,128)S(1)} %get-tuple-element.119), channel_id=1, source_target_pairs={{0,1},{1,2},{2,3},{3,4},{4,5},{5,6},{6,7},{8,9},{9,10},{10,11},{11... | collective-permute-start | bytes 196616 | tf_op jit(solution)/shard_map/ppermute | solution.py:14
  145.1 5.6 %collective-permute-start.14 = (f32[2,1,64,128]{3,2,1,0:T(8,128)S(1)}, f32[2,1,64,128]{3,2,1,0:T(8,128)S(1)}, u32[]{:S(2)}, u32[]{:S(2)}) collective-permute-start(f32[2,1,64,128]{3,2,1,0:T(8,128)S(1)} %get-tuple-element.120), channel_id=1, source_target_pairs={{1,0},{2,1},{3,2},{4,3},{5,4},{6,5},{7,6},{9,8},{10,9},{11,10},{12... | collective-permute-start | bytes 196616 | tf_op jit(solution)/shard_map/ppermute | solution.py:17
  150.7 1.0 copy-start.16
  151.2 1.1 copy-start.4
  151.2 1.2 copy-start.6
  151.2 1.4 copy-start.8
  151.2 1.5 copy-start.10
  151.2 1.7 copy-start.12
  151.2 1.8 copy-start.14
  153.1 1.2 copy-start.2
  158.5 5.8 %collective-permute-start.17 = (f32[1,1,64,128]{3,2,1,0:T(8,128)S(1)}, f32[1,1,64,128]{3,2,1,0:T(8,128)S(1)}, u32[]{:S(2)}, u32[]{:S(2)}) collective-permute-start(f32[1,1,64,128]{3,2,1,0:T(8,128)S(1)} %get-tuple-element.135), channel_id=1, source_target_pairs={{0,1},{1,2},{2,3},{3,4},{4,5},{5,6},{6,7},{8,9},{9,10},{10,11},{11... | collective-permute-start | bytes 98312 | tf_op jit(solution)/shard_map/ppermute | solution.py:14
  160.5 5.3 %collective-permute-start.16 = (f32[1,1,64,128]{3,2,1,0:T(8,128)S(1)}, f32[1,1,64,128]{3,2,1,0:T(8,128)S(1)}, u32[]{:S(2)}, u32[]{:S(2)}) collective-permute-start(f32[1,1,64,128]{3,2,1,0:T(8,128)S(1)} %get-tuple-element.136), channel_id=1, source_target_pairs={{1,0},{2,1},{3,2},{4,3},{5,4},{6,5},{7,6},{9,8},{10,9},{11,10},{12... | collective-permute-start | bytes 98312 | tf_op jit(solution)/shard_map/ppermute | solution.py:17
  164.3 112.9 %copy-start.18 = (f32[65536]{0:T(1024)}, f32[65536]{0:T(1024)S(1)}, u32[]{:S(2)}) copy-start(f32[65536]{0:T(1024)S(1)} %scatter_fusion.7) | copy-start | bytes 786436
  (8 other events, 6.7 us)
Sparse Core Ops, SparseCore 0:
  154.4 118.7 all-gather.1
where the time goes:
time: 318 us; the launch traced here: 317 us
  waiting for transfers between devices  127 us (40%)
  starting transfers between devices  79.8 us (25%)
  other arithmetic  37 us (12%)
  between operations  36.5 us (11%)
  blocking collectives  29 us (9%)
  local copies, waits for them, and re-layouts  7.28 us (2%)
    all_gather x1, waiting for transfers between devices, total_of_pieces(): return lax.all_gather(value, axis).sum(0)  107 us
    ppermute x9, starting transfers between devices, extended(): lax.ppermute(lax.slice_in_dim(block, 0, width, axis=dim), axis, backward)  59.6 us
    all_to_all x1, blocking collectives, sent_to_all(): lax.all_to_all(jnp.broadcast_to(value[None], (devices, *value.shape)), ax...  29 us
    ppermute x9, starting transfers between devices, extended(): lax.ppermute(lax.slice_in_dim(block, block.shape[dim] - width, None, axis...  20.2 us
    ppermute x9, waiting for transfers between devices, extended(): lax.ppermute(lax.slice_in_dim(block, 0, width, axis=dim), axis, backward)  19.8 us
    scatter-add x8, other arithmetic, inject(): flat = flat.at[rows, local].add(jnp.where(valid, values, 0.0))  11.4 us
  transfers between devices with their start and end apart: 19, of which 9 were waited for; matrix products, arithmetic and copies ran while one was open for 3% of the time, Pallas kernels for 0%

commit v1 on v0

v1 whole, which is shorter than its diff:
```python
import functools

import jax
import jax.numpy as jnp
from jax import lax
from jax.experimental import pallas as pl
from jax.experimental.pallas import tpu as pltpu
from jax.sharding import PartitionSpec as P

WINDOW = 8
PAD = 8
MESH = pl.DeviceIdType.MESH


def kernel(
    shape, iters, shots, slabs,
    wavelet, src_index, misfit_hbm, rec_hbm, model_hbm, un_hbm, ul_hbm, an_hbm, al_hbm,
    new_model_hbm, stepped_hbm, adjoint_hbm,
    now, mid, mod, lus, image, inj, src, onehot, misfit, rec,
    part, groups_sum, grad, peak_slab, peak_class, base, out_model, out_step,
    load_sem, halo_send, halo_recv, first_send, first_recv, far_sem, near_sem,
    rs_send, rs_recv, gs_send, gs_recv, ag_send, ag_recv, ps_send, ps_recv, pc_send, pc_recv, out_sem,
):
    depth, rows, cols = shape
    rounds = iters // 2
    me = lax.axis_index("shot")
    slab = lax.axis_index("slab")
    odd = lax.rem(slab, 2)
    body = pl.ds(PAD, rows)
    own = pl.ds(2, depth)

    def at_shot(offset):
        return {"shot": lax.rem(me + offset + shots, shots)}

    def at_slab(offset):
        return {"slab": lax.rem(slab + offset + slabs, slabs)}

    def signal(sem, device):
        pl.semaphore_signal(sem, inc=1, device_id=device, device_id_type=MESH)

    def remote(source, target, send, recv, device):
        return pltpu.make_async_remote_copy(
            src_ref=source, dst_ref=target, send_sem=send, recv_sem=recv, device_id=device, device_id_type=MESH
        )

    loads = [
        pltpu.make_async_copy(un_hbm.at[0], now.at[0, 0, own, body], load_sem.at[0]),
        pltpu.make_async_copy(an_hbm.at[0], now.at[0, 1, own, body], load_sem.at[1]),
        pltpu.make_async_copy(ul_hbm.at[0], mid.at[0, 0, own, body], load_sem.at[2]),
        pltpu.make_async_copy(al_hbm.at[0], mid.at[0, 1, own, body], load_sem.at[3]),
        pltpu.make_async_copy(model_hbm, mod.at[own], load_sem.at[4]),
        pltpu.make_async_copy(misfit_hbm.at[0], misfit, load_sem.at[5]),
        pltpu.make_async_copy(rec_hbm, rec, load_sem.at[6]),
    ]
    for copy in loads:
        copy.start()
    barrier = pltpu.get_barrier_semaphore()
    for offset in (1, -1):
        signal(barrier, at_slab(offset))
        signal(barrier, at_shot(offset))
    pl.semaphore_wait(barrier, 4)

    sides = (1 - odd, odd)

    def exists(side):
        return jnp.where(side == 0, slab > 0, slab < slabs - 1)

    def halo(rnd, field, side):
        return remote(
            now.at[rnd, field, pl.ds(2 + (depth - 2) * side, 2), body],
            now.at[rnd, field, pl.ds((depth + 2) * (1 - side), 2), body],
            halo_send.at[rnd, field, side], halo_recv.at[rnd, field, 1 - side],
            {"slab": slab + 2 * side - 1},
        )

    def halo_in(rnd, field, side):
        return remote(
            now.at[rnd, field, pl.ds(2 + (depth - 2) * side, 2), body],
            now.at[rnd, field, pl.ds((depth + 2) * side, 2), body],
            halo_send.at[rnd, field, side], halo_recv.at[rnd, field, side],
            {"slab": slab + 2 * side - 1},
        )

    def edge(side):
        return 2 + (depth - 1) * side

    def ghost(side):
        return 1 + (depth + 1) * side

    def first_refs(which, plane):
        if which == 2:
            return mod.at[pl.ds(plane, 1)]
        return mid.at[0, which, pl.ds(plane, 1), body]

    def first(which, side, target, arrival):
        return remote(
            first_refs(which, edge(side)), first_refs(which, ghost(target)),
            first_send.at[which, side], first_recv.at[which, arrival], {"slab": slab + 2 * side - 1},
        )

    def last(side, target, arrival):
        return remote(
            now.at[rounds, 0, pl.ds(edge(side), 1), body], now.at[rounds, 0, pl.ds(ghost(target), 1), body],
            halo_send.at[rounds, 0, side], halo_recv.at[rounds, 0, arrival], {"slab": slab + 2 * side - 1},
        )

    def on_sides(action):
        for side in sides:
            @pl.when(exists(side))
            def _():
                action(side)

    loads[0].wait()
    on_sides(lambda side: halo(0, 0, side).start())
    loads[2].wait()
    loads[4].wait()

    def send_first_u(side):
        first(0, side, 1 - side, 1 - side).start()
        first(2, side, 1 - side, 1 - side).start()

    on_sides(send_first_u)
    loads[1].wait()
    on_sides(lambda side: halo(0, 1, side).start())
    loads[3].wait()
    on_sides(lambda side: first(1, side, 1 - side, 1 - side).start())
    for offset in (1, -1):
        signal(far_sem.at[0], at_shot(offset))
        signal(near_sem.at[0], at_slab(offset))

    strip = jnp.zeros((PAD, cols), jnp.float32)
    plane0 = jnp.zeros((rows, cols), jnp.float32)

    def clear(plane, carry):
        for rnd in range(rounds + 1):
            for field in range(2):
                for ref in (now, mid):
                    ref[rnd, field, plane, 0:PAD, :] = strip
                    ref[rnd, field, plane, PAD + rows : PAD + rows + PAD, :] = strip
        image[plane] = plane0
        return carry

    lax.fori_loop(0, depth + 4, clear, 0)
    for side in range(2):
        @pl.when(jnp.logical_not(exists(side)))
        def _():
            for plane in range(2):
                at = (depth + 2) * side + plane
                mod[at] = plane0
                for field in range(2):
                    mid[0, field, at, body, :] = plane0
                    for rnd in range(rounds + 1):
                        now[rnd, field, at, body, :] = plane0

    loads[5].wait()
    loads[6].wait()
    line = lax.shift_right_logical(rec[...], 7)
    lane = jnp.bitwise_and(rec[...], cols - 1)
    src_line = lax.shift_right_logical(src_index[0], 7)
    src_lane = jnp.bitwise_and(src_index[0], cols - 1)
    row_id = lax.broadcasted_iota(jnp.int32, (rows, cols), 0)
    col_id = lax.broadcasted_iota(jnp.int32, (rows, cols), 1)

    def mark(plane, carry):
        here = row_id + (slab * depth + plane - 2) * rows
        hit = jnp.where(here == line, 1.0, 0.0).astype(jnp.bfloat16)
        at = pl.ds(pl.multiple_of(plane * rows, rows), rows)
        for copy in range(3):
            onehot[at, copy * cols : (copy + 1) * cols] = hit
        src[plane] = jnp.where((here == src_line) & (col_id == src_lane), 1.0, 0.0)
        return carry

    lax.fori_loop(1, depth + 3, mark, 0)
    cell_id = lax.broadcasted_iota(jnp.int32, (cols, cols), 0)

    def place(k, carry):
        value = jnp.where(cell_id == lane, misfit[pl.ds(k, 1), :], 0.0)
        high = value.astype(jnp.bfloat16)
        value = value - high.astype(jnp.float32)
        middle = value.astype(jnp.bfloat16)
        value = value - middle.astype(jnp.float32)
        pieces = jnp.concatenate([high, middle, value.astype(jnp.bfloat16)], axis=1)
        added = lax.dot_general(
            onehot[rows : (depth + 3) * rows, :], pieces, (((1,), (1,)), ((), ())), preferred_element_type=jnp.float32
        )
        inj[k, 1 : depth + 3] = added.reshape(depth + 2, rows, cols)
        return carry

    lax.fori_loop(0, iters, place, 0)

    first_lane = col_id == 0
    last_lane = col_id == cols - 1

    def laplace(ref, plane, center):
        left = jnp.where(first_lane, 0.0, pltpu.roll(center, 1, 1))
        right = jnp.where(last_lane, 0.0, pltpu.roll(center, cols - 1, 1))
        beside = ref[plane + 1, body, :] + ref[plane - 1, body, :]
        beside = beside + (ref[plane, PAD + 1 : PAD + 1 + rows, :] + ref[plane, PAD - 1 : PAD - 1 + rows, :])
        return beside + (left + right) - 6.0 * center

    def advance(field, state, later, target, start, count, k, slot):
        def one(index, carry):
            plane = start + index
            center = state[plane, body, :]
            lap = laplace(state, plane, center)
            fresh = 2.0 * center - later[plane, body, :] + mod[plane] * lap
            if field == 0:
                lus[slot, plane] = lap
                fresh = fresh + wavelet[0, k] * src[plane]
            else:
                image[plane] = image[plane] + center * lus[slot, plane]
                fresh = fresh + inj[k, plane]
            target[plane, body, :] = fresh
            return carry

        lax.fori_loop(0, count, one, 0)

    def both_steps(rnd, field, first_at, first_count, second_at, second_count):
        a, b, c, d = now.at[rnd, field], mid.at[rnd, field], mid.at[rnd + 1, field], now.at[rnd + 1, field]
        advance(field, a, b, c, first_at, first_count, 2 * rnd, 0)
        advance(field, c, a, d, second_at, second_count, 2 * rnd + 1, 1)

    for rnd in range(rounds):
        for field in range(2):
            if rnd == 0 and field == 0:
                pass
            both_steps(rnd, field, 3, depth - 2, 4, depth - 4)
        for side in sides:
            for field in range(2):
                @pl.when(exists(side))
                def _():
                    halo_in(rnd, field, side).wait_recv()
                    if rnd == 0:
                        first(field, side, side, side).wait_recv()
                        if field == 0:
                            first(2, side, side, side).wait_recv()

                both_steps(rnd, field, 1 + depth * side, 2, 2 + (depth - 2) * side, 2)

                @pl.when(exists(side))
                def _():
                    if rnd + 1 < rounds:
                        halo(rnd + 1, field, side).start()
                    elif field == 0:
                        last(side, 1 - side, 1 - side).start()
        if rnd < 3:
            pl.semaphore_wait(far_sem.at[rnd], 2)
            for offset in (2 << rnd, -(2 << rnd)):
                signal(far_sem.at[rnd + 1], at_shot(offset))
        if rnd < 2:
            pl.semaphore_wait(near_sem.at[rnd], 2)
        if rnd == 0:
            for offset in (2, -2):
                signal(near_sem.at[1], at_slab(offset))

    far = jnp.where(odd == 0, WINDOW // 2, -(WINDOW // 2))
    offsets = [far] + [sign * step for step in range(WINDOW // 2 - 1, 0, -1) for sign in (1, -1)]
    height = rows // WINDOW
    my_class = lax.rem(me, WINDOW)
    my_group = lax.div(me, WINDOW)
    count = shots // WINDOW

    def class_rows(which):
        return pl.ds(pl.multiple_of(which * height, height), height)

    scatter = []
    for slot, offset in enumerate(offsets):
        theirs = lax.rem(me + offset + shots, WINDOW)
        copy = remote(
            image.at[own, class_rows(theirs)], part.at[slot], rs_send.at[slot], rs_recv.at[slot], at_shot(offset)
        )
        copy.start()
        scatter.append(copy)
    adjoint_out = pltpu.make_async_copy(now.at[rounds, 1, own, body], adjoint_hbm.at[0], out_sem.at[0])
    adjoint_out.start()
    for copy in reversed(scatter):
        copy.wait_recv()

    def gather_window(plane, carry):
        total = image[plane + 2, class_rows(my_class), :]
        for slot in range(len(offsets)):
            total = total + part[slot, plane]
        groups_sum[my_group, plane] = total
        return carry

    lax.fori_loop(0, depth, gather_window, 0)
    pl.semaphore_wait(far_sem.at[3], 2)
    exchange = []
    for turn in (2, 1, 3):
        other = lax.rem(my_group + turn, count)
        copy = remote(
            groups_sum.at[my_group], groups_sum.at[my_group], gs_send.at[turn], gs_recv.at[turn], at_shot(turn * WINDOW)
        )
        copy.start()
        exchange.append((copy, other))

    def wait_last(side):
        last(side, side, side).wait_recv()

    on_sides(wait_last)

    def prepare(plane, carry):
        state = now.at[rounds, 0]
        center = state[plane, body, :]
        lus[0, plane] = laplace(state, plane, center)
        base[plane - 2] = 2.0 * center - mid[rounds, 0, plane, body, :]
        return carry

    lax.fori_loop(2, depth + 2, prepare, 0)
    for turn, (copy, other) in zip((2, 1, 3), exchange):
        origin = lax.rem(my_group + count - turn, count)
        remote(
            groups_sum.at[my_group], groups_sum.at[origin], gs_send.at[turn], gs_recv.at[turn], at_shot(turn * WINDOW)
        ).wait_recv()

    def finish(plane, carry):
        total = groups_sum[0, plane]
        for group in range(1, count):
            total = total + groups_sum[group, plane]
        grad[plane, class_rows(my_class), :] = total
        return jnp.maximum(carry, jnp.abs(total))

    top = lax.fori_loop(0, depth, finish, jnp.zeros((height, cols), jnp.float32))
    peak_slab[slab] = top
    peaks = []
    for turn in range(1, slabs):
        copy = remote(peak_slab.at[slab], peak_slab.at[slab], ps_send.at[turn], ps_recv.at[turn], at_slab(turn))
        copy.start()
        peaks.append(copy)
    gather = []
    for slot, offset in enumerate(offsets):
        mine = grad.at[:, class_rows(my_class)]
        copy = remote(mine, mine, ag_send.at[slot], ag_recv.at[slot], at_shot(offset))
        copy.start()
        gather.append(copy)
    for turn in range(1, slabs):
        origin = lax.rem(slab + slabs - turn, slabs)
        remote(
            peak_slab.at[slab], peak_slab.at[origin], ps_send.at[turn], ps_recv.at[turn], at_slab(turn)
        ).wait_recv()
    top = peak_slab[0]
    for other in range(1, slabs):
        top = jnp.maximum(top, peak_slab[other])
    peak_class[my_class] = top
    class_peaks = []
    for slot, offset in enumerate(offsets):
        copy = remote(
            peak_class.at[my_class], peak_class.at[my_class], pc_send.at[slot], pc_recv.at[slot], at_shot(offset)
        )
        copy.start()
        class_peaks.append(copy)
    for slot, offset in enumerate(offsets):
        origin = lax.rem(me - offset + shots, WINDOW)
        theirs = grad.at[:, class_rows(origin)]
        remote(theirs, theirs, ag_send.at[slot], ag_recv.at[slot], at_shot(offset)).wait_recv()
        remote(
            peak_class.at[origin], peak_class.at[origin], pc_send.at[slot], pc_recv.at[slot], at_shot(offset)
        ).wait_recv()
    top = peak_class[0]
    for other in range(1, WINDOW):
        top = jnp.maximum(top, peak_class[other])
    peak = jnp.max(jnp.max(top, axis=0, keepdims=True), axis=1, keepdims=True) + 1e-6

    def update(plane, carry):
        fresh = jnp.clip(mod[plane + 2] - 0.1 * grad[plane] / peak, 0.05, 0.3)
        out_model[plane] = fresh
        out_step[plane] = base[plane] + fresh * lus[0, plane + 2]
        return carry

    lax.fori_loop(0, depth, update, 0)
    outs = [
        pltpu.make_async_copy(out_model, new_model_hbm, out_sem.at[1]),
        pltpu.make_async_copy(out_step, stepped_hbm.at[0], out_sem.at[2]),
    ]
    for copy in outs:
        copy.start()

    def sent(side):
        for field in range(2):
            for rnd in range(rounds):
                halo(rnd, field, side).wait_send()
        last(side, 1 - side, 1 - side).wait_send()
        for which in range(3):
            first(which, side, 1 - side, 1 - side).wait_send()

    on_sides(sent)
    for copy in scatter + [pair[0] for pair in exchange] + peaks + gather + class_peaks:
        copy.wait_send()
    adjoint_out.wait()
    for copy in outs:
        copy.wait()


def solution(mesh):
    shots, slabs = mesh.shape["shot"], mesh.shape["slab"]

    def per_device(model, fwd_now, fwd_next, adj_now, adj_next, wavelet, misfit, src_index, rec_index):
        shape = model.shape
        depth, rows, cols = shape
        iters, receivers = misfit.shape[1:]
        rounds = iters // 2
        f32 = jnp.float32
        dma = pltpu.SemaphoreType.DMA
        height = rows // WINDOW
        smem = pl.BlockSpec(memory_space=pltpu.SMEM)
        hbm = pl.BlockSpec(memory_space=pl.ANY)
        return pl.pallas_call(
            functools.partial(kernel, shape, iters, shots, slabs),
            out_shape=(
                jax.ShapeDtypeStruct(shape, f32),
                jax.ShapeDtypeStruct(fwd_now.shape, f32),
                jax.ShapeDtypeStruct(adj_now.shape, f32),
            ),
            in_specs=[smem, smem] + [hbm] * 7,
            out_specs=(hbm, hbm, hbm),
            scratch_shapes=[
                pltpu.VMEM((rounds + 1, 2, depth + 4, rows + 2 * PAD, cols), f32),
                pltpu.VMEM((rounds + 1, 2, depth + 4, rows + 2 * PAD, cols), f32),
                pltpu.VMEM((depth + 4, rows, cols), f32),
                pltpu.VMEM((2, depth + 4, rows, cols), f32),
                pltpu.VMEM((depth + 4, rows, cols), f32),
                pltpu.VMEM((iters, depth + 4, rows, cols), f32),
                pltpu.VMEM((depth + 4, rows, cols), f32),
                pltpu.VMEM(((depth + 4) * rows, 3 * receivers), jnp.bfloat16),
                pltpu.VMEM((iters, receivers), f32),
                pltpu.VMEM((1, receivers), jnp.int32),
                pltpu.VMEM((WINDOW - 1, depth, height, cols), f32),
                pltpu.VMEM((shots // WINDOW, depth, height, cols), f32),
                pltpu.VMEM(shape, f32),
                pltpu.VMEM((slabs, height, cols), f32),
                pltpu.VMEM((WINDOW, height, cols), f32),
                pltpu.VMEM(shape, f32),
                pltpu.VMEM(shape, f32),
                pltpu.VMEM(shape, f32),
                dma((7,)),
                dma((rounds + 1, 2, 2)), dma((rounds + 1, 2, 2)),
                dma((3, 2)), dma((3, 2)),
                pltpu.SemaphoreType.REGULAR((4,)), pltpu.SemaphoreType.REGULAR((2,)),
                dma((WINDOW - 1,)), dma((WINDOW - 1,)),
                dma((shots // WINDOW,)), dma((shots // WINDOW,)),
                dma((WINDOW - 1,)), dma((WINDOW - 1,)),
                dma((slabs,)), dma((slabs,)),
                dma((WINDOW - 1,)), dma((WINDOW - 1,)),
                dma((3,)),
            ],
            compiler_params=pltpu.CompilerParams(
                collective_id=0, has_side_effects=True, vmem_limit_bytes=48 * 1024 * 1024
            ),
            name="reverse_time",
        )(wavelet, src_index, misfit, rec_index, model, fwd_now, fwd_next, adj_now, adj_next)

    field = P(("groups", "shot"), "slab", None, None)
    model_spec = P(("groups", "slab"), None, None)
    return jax.shard_map(
        per_device,
        mesh=mesh,
        in_specs=(
            model_spec, field, field, field, field,
            P(("groups", "shot"), None), P(("groups", "shot"), None, None), P(("groups", "shot")),
            P(("groups", "shot"), None),
        ),
        out_specs=(model_spec, field, field),
        check_vma=False,
    )
```

time: 318 us -> 105 us (0.33)
  waiting for transfers between devices: 127 us -> 0 us
  Pallas kernels: 0 us -> 96 us
  starting transfers between devices: 79.8 us -> 0 us
  other arithmetic: 37 us -> 0 us
  between operations: 36.5 us -> 1.35 us
  blocking collectives: 29 us -> 0 us
    all_gather x1 -> x0, waiting for transfers between devices: 107 us -> none  [total_of_pieces(): return lax.all_gather(value, axis).sum(0)]
    pallas_call x0 -> x1, Pallas kernels: none -> 96 us  [per_device(): pl.pallas_call(functools.partial(kernel, shape, iters, shots, slabs), out...]
    ppermute x18 -> x0, starting transfers between devices: 79.8 us -> none  [the longest x9 59.6 us: extended(): lax.ppermute(lax.slice_in_dim(block, 0, width, axis=dim), axis, backward)]
    all_to_all x1 -> x0, blocking collectives: 29 us -> none  [sent_to_all(): lax.all_to_all(jnp.broadcast_to(value[None], (devices, *value.shape)), ax...]
    ppermute x18 -> x0, waiting for transfers between devices: 19.8 us -> none  [the longest x9 19.8 us: extended(): lax.ppermute(lax.slice_in_dim(block, 0, width, axis=dim), axis, backward)]
    scatter-add x8 -> x0, other arithmetic: 11.4 us -> none  [inject(): flat = flat.at[rows, local].add(jnp.where(valid, values, 0.0))]
    add x18 -> x0, other arithmetic: 9.44 us -> none  [the longest x8 5.19 us: inject(): flat = flat.at[rows, local].add(jnp.where(valid, values, 0.0))]
    unnamed x43 -> x19, local copies, waits for them, and re-layouts: 3.09 us -> 7.55 us
  transfers between devices with their start and end apart: 19 -> 0, of which waited for: 9 -> 0; matrix products, arithmetic and copies ran while one was open for 3% -> 0% of each run, Pallas kernels for 0% -> 0%
where the time goes in v1:
time: 105 us
  Pallas kernels  96 us (91%)
  local copies, waits for them, and re-layouts  7.55 us (7%)
  between operations  1.35 us (1%)
    pallas_call x1, Pallas kernels, per_device(): pl.pallas_call(functools.partial(kernel, shape, iters, shots, slabs), out...  96 us
    unnamed x19, local copies, waits for them, and re-layouts  7.55 us

profile of v1, /device:TPU:33, one launch (start us, length us, event | category | flops | bytes accessed | tf_op | source)
XLA Modules:
  0.0 104.9 jit_solution(16248719480564338647)
XLA Ops:
  0.6 0.0 copy-start.7
  0.6 0.0 copy-start.6
  1.3 0.0 copy-done.7
  1.3 0.0 copy-done.6
  1.3 0.0 copy-start
  1.3 0.9 copy-done
  2.3 0.0 copy-start.1
  2.3 0.9 copy-done.1
  3.2 0.0 copy-start.2
  3.2 0.9 copy-done.2
  4.2 0.0 copy-start.3
  4.2 0.9 copy-done.3
  5.1 0.0 copy-start.4
  5.1 0.9 copy-done.4
  6.1 0.0 copy-start.5
  6.1 0.7 copy-done.5
  6.8 96.0 %reverse_time.1 = (f32[8,64,128]{2,1,0:T(8,128)S(1)}, f32[1,8,64,128]{3,2,1,0:T(8,128)S(1)}, f32[1,8,64,128]{3,2,1,0:T(8,128)S(1)}) custom-call(f32[1,8]{1,0:T(1,128)S(1)} %copy-done.6, s32[1]{0:T(128)S(6)} %copy.15.src_index, f32[1,8,128]{2,1,0:T(8,128)S(1)} %copy-done.5, s32[1,128]{1,0:T(1,128)S(1)} %copy-done.7, f32[8,64,128]{2,1,0:T(8,128)S(1)} %copy-done, ...), custom_call_target="tpu_custom_call" | custom-call | tf_op jit(solution)/shard_map/reverse_time/pallas_call | solution.py:407
  102.8 0.7 copy.16
  103.5 0.7 copy.17
  104.2 0.7 copy.18
Async XLA Ops:
  0.6 0.7 copy-start.7
  0.6 0.7 copy-start.6
  1.3 1.0 copy-start
  2.3 0.9 copy-start.1
  3.2 0.9 copy-start.2
  4.2 0.9 copy-start.3
  5.1 0.9 copy-start.4
  6.1 0.7 copy-start.5

commit v2 on v1

--- a/solution.py
+++ b/solution.py
@@ -14,12 +14,12 @@
 
 def kernel(
     shape, iters, shots, slabs,
-    wavelet, src_index, misfit_hbm, rec_hbm, model_hbm, un_hbm, ul_hbm, an_hbm, al_hbm,
-    new_model_hbm, stepped_hbm, adjoint_hbm,
-    now, mid, mod, lus, image, inj, src, onehot, misfit, rec,
-    part, groups_sum, grad, peak_slab, peak_class, base, out_model, out_step,
+    src_index, wavelet_hbm, misfit_hbm, rec_hbm, model_hbm, un_hbm, ul_hbm, an_hbm, al_hbm,
+    grad_out, peak_out, model_out, base_out, lap_out, adjoint_out,
+    now, mid, mod, lus, image, inj, src, onehot, misfit, rec, wavelet,
+    part, groups_sum, grad, peak_slab, peak_class,
     load_sem, halo_send, halo_recv, first_send, first_recv, far_sem, near_sem,
-    rs_send, rs_recv, gs_send, gs_recv, ag_send, ag_recv, ps_send, ps_recv, pc_send, pc_recv, out_sem,
+    rs_send, rs_recv, gs_send, gs_recv, relay_send, relay_recv, ag_send, ag_recv, ps_send, ps_recv, pc_send, pc_recv,
 ):
     depth, rows, cols = shape
     rounds = iters // 2
@@ -51,6 +51,7 @@
         pltpu.make_async_copy(model_hbm, mod.at[own], load_sem.at[4]),
         pltpu.make_async_copy(misfit_hbm.at[0], misfit, load_sem.at[5]),
         pltpu.make_async_copy(rec_hbm, rec, load_sem.at[6]),
+        pltpu.make_async_copy(wavelet_hbm, wavelet, load_sem.at[7]),
     ]
     for copy in loads:
         copy.start()
@@ -152,8 +153,8 @@
                     for rnd in range(rounds + 1):
                         now[rnd, field, at, body, :] = plane0
 
-    loads[5].wait()
-    loads[6].wait()
+    for copy in loads[5:]:
+        copy.wait()
     line = lax.shift_right_logical(rec[...], 7)
     lane = jnp.bitwise_and(rec[...], cols - 1)
     src_line = lax.shift_right_logical(src_index[0], 7)
@@ -220,11 +221,37 @@
         advance(field, a, b, c, first_at, first_count, 2 * rnd, 0)
         advance(field, c, a, d, second_at, second_count, 2 * rnd + 1, 1)
 
+    far = jnp.where(odd == 0, WINDOW // 2, -(WINDOW // 2))
+    offsets = [far] + [sign * step for step in range(WINDOW // 2 - 1, 0, -1) for sign in (1, -1)]
+    height = rows // WINDOW
+    my_class = lax.rem(me, WINDOW)
+    my_group = lax.div(me, WINDOW)
+    count = shots // WINDOW
+    half = depth // 2
+    sends = []
+
+    def class_rows(which):
+        return pl.ds(pl.multiple_of(which * height, height), height)
+
+    def scatter(piece, source, length, target):
+        copies = []
+        for slot, offset in enumerate(offsets):
+            theirs = lax.rem(me + offset + shots, WINDOW)
+            copy = remote(
+                image.at[pl.ds(source, length), class_rows(theirs)], part.at[slot, pl.ds(target, length)],
+                rs_send.at[piece, slot], rs_recv.at[piece, slot], at_shot(offset),
+            )
+            copy.start()
+            copies.append(copy)
+        sends.extend(copies)
+        return copies
+
+    scattered = [[], []]
     for rnd in range(rounds):
         for field in range(2):
-            if rnd == 0 and field == 0:
-                pass
             both_steps(rnd, field, 3, depth - 2, 4, depth - 4)
+        if rnd + 1 == rounds:
+            scattered[0] += scatter(0, 4, half, 0)
         for side in sides:
             for field in range(2):
                 @pl.when(exists(side))
@@ -237,6 +264,9 @@
 
                 both_steps(rnd, field, 1 + depth * side, 2, 2 + (depth - 2) * side, 2)
 
+                if rnd + 1 == rounds and field == 1:
+                    scattered[1] += scatter(1 + side, 2 + (depth - 2) * side, 2, half + 2 * side)
+
                 @pl.when(exists(side))
                 def _():
                     if rnd + 1 < rounds:
@@ -245,135 +275,118 @@
                         last(side, 1 - side, 1 - side).start()
         if rnd < 3:
             pl.semaphore_wait(far_sem.at[rnd], 2)
+        if rnd < 2:
             for offset in (2 << rnd, -(2 << rnd)):
                 signal(far_sem.at[rnd + 1], at_shot(offset))
-        if rnd < 2:
             pl.semaphore_wait(near_sem.at[rnd], 2)
         if rnd == 0:
             for offset in (2, -2):
                 signal(near_sem.at[1], at_slab(offset))
 
-    far = jnp.where(odd == 0, WINDOW // 2, -(WINDOW // 2))
-    offsets = [far] + [sign * step for step in range(WINDOW // 2 - 1, 0, -1) for sign in (1, -1)]
-    height = rows // WINDOW
-    my_class = lax.rem(me, WINDOW)
-    my_group = lax.div(me, WINDOW)
-    count = shots // WINDOW
-
-    def class_rows(which):
-        return pl.ds(pl.multiple_of(which * height, height), height)
-
-    scatter = []
-    for slot, offset in enumerate(offsets):
-        theirs = lax.rem(me + offset + shots, WINDOW)
-        copy = remote(
-            image.at[own, class_rows(theirs)], part.at[slot], rs_send.at[slot], rs_recv.at[slot], at_shot(offset)
-        )
-        copy.start()
-        scatter.append(copy)
-    adjoint_out = pltpu.make_async_copy(now.at[rounds, 1, own, body], adjoint_hbm.at[0], out_sem.at[0])
-    adjoint_out.start()
-    for copy in reversed(scatter):
-        copy.wait_recv()
-
-    def gather_window(plane, carry):
-        total = image[plane + 2, class_rows(my_class), :]
-        for slot in range(len(offsets)):
-            total = total + part[slot, plane]
-        groups_sum[my_group, plane] = total
-        return carry
-
-    lax.fori_loop(0, depth, gather_window, 0)
-    pl.semaphore_wait(far_sem.at[3], 2)
-    exchange = []
-    for turn in (2, 1, 3):
-        other = lax.rem(my_group + turn, count)
-        copy = remote(
-            groups_sum.at[my_group], groups_sum.at[my_group], gs_send.at[turn], gs_recv.at[turn], at_shot(turn * WINDOW)
-        )
-        copy.start()
-        exchange.append((copy, other))
-
-    def wait_last(side):
-        last(side, side, side).wait_recv()
-
-    on_sides(wait_last)
+    def at_group(turn):
+        return lax.rem(my_group + turn + count, count)
+
+    def passed(piece, turn):
+        start = half * piece
+        mine = groups_sum.at[my_group, pl.ds(start, half)]
+        return remote(
+            mine, mine, gs_send.at[piece, turn], gs_recv.at[piece, turn], at_shot(WINDOW if turn else -WINDOW)
+        )
+
+    def passed_in(piece, turn):
+        start = half * piece
+        origin = at_group(-1 if turn else 1)
+        theirs = groups_sum.at[origin, pl.ds(start, half)]
+        return remote(
+            theirs, theirs, gs_send.at[piece, turn], gs_recv.at[piece, turn], at_shot(WINDOW if turn else -WINDOW)
+        )
+
+    def relayed(piece, turn, origin):
+        start = half * piece + (half // 2) * (1 - turn)
+        theirs = groups_sum.at[origin, pl.ds(start, half // 2)]
+        return remote(
+            theirs, theirs, relay_send.at[piece, turn], relay_recv.at[piece, turn], at_shot(WINDOW if turn else -WINDOW)
+        )
+
+    for piece in range(2):
+        for copy in scattered[piece]:
+            copy.wait_recv()
+        for slot in range(half * piece, half * (piece + 1)):
+            plane = slot + 4 if piece == 0 else (slot - half + 2 if slot < half + 2 else slot + 2)
+            total = image[plane, class_rows(my_class), :]
+            for index in range(len(offsets)):
+                total = total + part[index, slot]
+            groups_sum[my_group, slot] = total
+        for turn in range(2):
+            copy = passed(piece, turn)
+            copy.start()
+            sends.append(copy)
+
+    on_sides(lambda side: last(side, side, side).wait_recv())
 
     def prepare(plane, carry):
         state = now.at[rounds, 0]
         center = state[plane, body, :]
-        lus[0, plane] = laplace(state, plane, center)
-        base[plane - 2] = 2.0 * center - mid[rounds, 0, plane, body, :]
+        lap_out[plane - 2] = laplace(state, plane, center)
+        base_out[plane - 2] = 2.0 * center - mid[rounds, 0, plane, body, :]
+        adjoint_out[plane - 2] = now[rounds, 1, plane, body, :]
+        model_out[plane - 2] = mod[plane]
         return carry
 
     lax.fori_loop(2, depth + 2, prepare, 0)
-    for turn, (copy, other) in zip((2, 1, 3), exchange):
-        origin = lax.rem(my_group + count - turn, count)
-        remote(
-            groups_sum.at[my_group], groups_sum.at[origin], gs_send.at[turn], gs_recv.at[turn], at_shot(turn * WINDOW)
-        ).wait_recv()
-
-    def finish(plane, carry):
-        total = groups_sum[0, plane]
-        for group in range(1, count):
-            total = total + groups_sum[group, plane]
-        grad[plane, class_rows(my_class), :] = total
-        return jnp.maximum(carry, jnp.abs(total))
-
-    top = lax.fori_loop(0, depth, finish, jnp.zeros((height, cols), jnp.float32))
-    peak_slab[slab] = top
-    peaks = []
+    for piece in range(2):
+        for turn in range(2):
+            passed_in(piece, turn).wait_recv()
+            copy = relayed(piece, turn, at_group(-1 if turn else 1))
+            copy.start()
+            sends.append(copy)
+
+    top = jnp.zeros((height, cols), jnp.float32)
+    for piece in range(2):
+        for turn in range(2):
+            relayed(piece, turn, at_group(2)).wait_recv()
+        for slot in range(half * piece, half * (piece + 1)):
+            total = groups_sum[0, slot]
+            for group in range(1, count):
+                total = total + groups_sum[group, slot]
+            grad[slot, class_rows(my_class), :] = total
+            top = jnp.maximum(top, jnp.abs(total))
+        if piece == 1:
+            peak_slab[slab] = top
+            for turn in range(1, slabs):
+                copy = remote(peak_slab.at[slab], peak_slab.at[slab], ps_send.at[turn], ps_recv.at[turn], at_slab(turn))
+                copy.start()
+                sends.append(copy)
+        for slot, offset in enumerate(offsets):
+            mine = grad.at[pl.ds(half * piece, half), class_rows(my_class)]
+            copy = remote(mine, mine, ag_send.at[piece, slot], ag_recv.at[piece, slot], at_shot(offset))
+            copy.start()
+            sends.append(copy)
     for turn in range(1, slabs):
-        copy = remote(peak_slab.at[slab], peak_slab.at[slab], ps_send.at[turn], ps_recv.at[turn], at_slab(turn))
-        copy.start()
-        peaks.append(copy)
-    gather = []
-    for slot, offset in enumerate(offsets):
-        mine = grad.at[:, class_rows(my_class)]
-        copy = remote(mine, mine, ag_send.at[slot], ag_recv.at[slot], at_shot(offset))
-        copy.start()
-        gather.append(copy)
-    for turn in range(1, slabs):
-        origin = lax.rem(slab + slabs - turn, slabs)
-        remote(
-            peak_slab.at[slab], peak_slab.at[origin], ps_send.at[turn], ps_recv.at[turn], at_slab(turn)
-        ).wait_recv()
+        theirs = peak_slab.at[lax.rem(slab + slabs - turn, slabs)]
+        remote(theirs, theirs, ps_send.at[turn], ps_recv.at[turn], at_slab(turn)).wait_recv()
     top = peak_slab[0]
     for other in range(1, slabs):
         top = jnp.maximum(top, peak_slab[other])
     peak_class[my_class] = top
-    class_peaks = []
     for slot, offset in enumerate(offsets):
-        copy = remote(
-            peak_class.at[my_class], peak_class.at[my_class], pc_send.at[slot], pc_recv.at[slot], at_shot(offset)
-        )
+        mine = peak_class.at[my_class]
+        copy = remote(mine, mine, pc_send.at[slot], pc_recv.at[slot], at_shot(offset))
         copy.start()
-        class_peaks.append(copy)
+        sends.append(copy)
+    for piece in range(2):
+        for slot, offset in enumerate(offsets):
+            theirs = grad.at[pl.ds(half * piece, half), class_rows(lax.rem(me - offset + shots, WINDOW))]
+            remote(theirs, theirs, ag_send.at[piece, slot], ag_recv.at[piece, slot], at_shot(offset)).wait_recv()
+        for slot in range(half * piece, half * (piece + 1)):
+            grad_out[slot] = grad[slot]
     for slot, offset in enumerate(offsets):
-        origin = lax.rem(me - offset + shots, WINDOW)
-        theirs = grad.at[:, class_rows(origin)]
-        remote(theirs, theirs, ag_send.at[slot], ag_recv.at[slot], at_shot(offset)).wait_recv()
-        remote(
-            peak_class.at[origin], peak_class.at[origin], pc_send.at[slot], pc_recv.at[slot], at_shot(offset)
-        ).wait_recv()
+        theirs = peak_class.at[lax.rem(me - offset + shots, WINDOW)]
+        remote(theirs, theirs, pc_send.at[slot], pc_recv.at[slot], at_shot(offset)).wait_recv()
     top = peak_class[0]
     for other in range(1, WINDOW):
         top = jnp.maximum(top, peak_class[other])
-    peak = jnp.max(jnp.max(top, axis=0, keepdims=True), axis=1, keepdims=True) + 1e-6
-
-    def update(plane, carry):
-        fresh = jnp.clip(mod[plane + 2] - 0.1 * grad[plane] / peak, 0.05, 0.3)
-        out_model[plane] = fresh
-        out_step[plane] = base[plane] + fresh * lus[0, plane + 2]
-        return carry
-
-    lax.fori_loop(0, depth, update, 0)
-    outs = [
-        pltpu.make_async_copy(out_model, new_model_hbm, out_sem.at[1]),
-        pltpu.make_async_copy(out_step, stepped_hbm.at[0], out_sem.at[2]),
-    ]
-    for copy in outs:
-        copy.start()
+    peak_out[...] = top
 
     def sent(side):
         for field in range(2):
@@ -384,10 +397,35 @@
             first(which, side, 1 - side, 1 - side).wait_send()
 
     on_sides(sent)
-    for copy in scatter + [pair[0] for pair in exchange] + peaks + gather + class_peaks:
+    for copy in sends:
         copy.wait_send()
-    adjoint_out.wait()
-    for copy in outs:
+
+
+def update(shape, grad, top, model, base, lap, adjoint, new_model_hbm, stepped_hbm, adjoint_hbm, fresh_all, step_all, sem):
+    depth = shape[0]
+    half = depth // 2
+    kept = pltpu.make_async_copy(adjoint, adjoint_hbm.at[0], sem.at[0])
+    kept.start()
+    peak = jnp.max(jnp.max(top[...], axis=0, keepdims=True), axis=1, keepdims=True) + 1e-6
+    copies = [kept]
+    for slot in range(depth):
+        plane = slot + 2 if slot < half else (slot - half if slot < half + 2 else slot)
+        fresh = jnp.clip(model[plane] - 0.1 * grad[slot] / peak, 0.05, 0.3)
+        fresh_all[plane] = fresh
+        step_all[plane] = base[plane] + fresh * lap[plane]
+        if slot == half - 1:
+            planes = pl.ds(2, half)
+        elif slot == half + 1:
+            planes = pl.ds(0, 2)
+        elif slot == depth - 1:
+            planes = pl.ds(depth - 2, 2)
+        else:
+            continue
+        for source, target in ((fresh_all, new_model_hbm), (step_all, stepped_hbm.at[0])):
+            copy = pltpu.make_async_copy(source.at[planes], target.at[planes], sem.at[len(copies)])
+            copy.start()
+            copies.append(copy)
+    for copy in copies:
         copy.wait()
 
 
@@ -402,17 +440,15 @@
         f32 = jnp.float32
         dma = pltpu.SemaphoreType.DMA
         height = rows // WINDOW
-        smem = pl.BlockSpec(memory_space=pltpu.SMEM)
         hbm = pl.BlockSpec(memory_space=pl.ANY)
-        return pl.pallas_call(
+        vmem = pl.BlockSpec(memory_space=pltpu.VMEM)
+        whole = jax.ShapeDtypeStruct(shape, f32)
+        arguments = (wavelet, misfit, rec_index, model, fwd_now, fwd_next, adj_now, adj_next)
+        results = pl.pallas_call(
             functools.partial(kernel, shape, iters, shots, slabs),
-            out_shape=(
-                jax.ShapeDtypeStruct(shape, f32),
-                jax.ShapeDtypeStruct(fwd_now.shape, f32),
-                jax.ShapeDtypeStruct(adj_now.shape, f32),
-            ),
-            in_specs=[smem, smem] + [hbm] * 7,
-            out_specs=(hbm, hbm, hbm),
+            out_shape=(whole, jax.ShapeDtypeStruct((height, cols), f32), whole, whole, whole, whole),
+            in_specs=[pl.BlockSpec(memory_space=pltpu.SMEM)] + [hbm] * 8,
+            out_specs=(vmem,) * 6,
             scratch_shapes=[
                 pltpu.VMEM((rounds + 1, 2, depth + 4, rows + 2 * PAD, cols), f32),
                 pltpu.VMEM((rounds + 1, 2, depth + 4, rows + 2 * PAD, cols), f32),
@@ -424,30 +460,39 @@
                 pltpu.VMEM(((depth + 4) * rows, 3 * receivers), jnp.bfloat16),
                 pltpu.VMEM((iters, receivers), f32),
                 pltpu.VMEM((1, receivers), jnp.int32),
+                pltpu.SMEM((1, iters), f32),
                 pltpu.VMEM((WINDOW - 1, depth, height, cols), f32),
                 pltpu.VMEM((shots // WINDOW, depth, height, cols), f32),
                 pltpu.VMEM(shape, f32),
                 pltpu.VMEM((slabs, height, cols), f32),
                 pltpu.VMEM((WINDOW, height, cols), f32),
-                pltpu.VMEM(shape, f32),
-                pltpu.VMEM(shape, f32),
-                pltpu.VMEM(shape, f32),
-                dma((7,)),
+                dma((8,)),
                 dma((rounds + 1, 2, 2)), dma((rounds + 1, 2, 2)),
                 dma((3, 2)), dma((3, 2)),
-                pltpu.SemaphoreType.REGULAR((4,)), pltpu.SemaphoreType.REGULAR((2,)),
-                dma((WINDOW - 1,)), dma((WINDOW - 1,)),
-                dma((shots // WINDOW,)), dma((shots // WINDOW,)),
-                dma((WINDOW - 1,)), dma((WINDOW - 1,)),
+                pltpu.SemaphoreType.REGULAR((3,)), pltpu.SemaphoreType.REGULAR((2,)),
+                dma((3, WINDOW - 1)), dma((3, WINDOW - 1)),
+                dma((2, 2)), dma((2, 2)),
+                dma((2, 2)), dma((2, 2)),
+                dma((2, WINDOW - 1)), dma((2, WINDOW - 1)),
                 dma((slabs,)), dma((slabs,)),
                 dma((WINDOW - 1,)), dma((WINDOW - 1,)),
-                dma((3,)),
             ],
             compiler_params=pltpu.CompilerParams(
                 collective_id=0, has_side_effects=True, vmem_limit_bytes=48 * 1024 * 1024
             ),
             name="reverse_time",
-        )(wavelet, src_index, misfit, rec_index, model, fwd_now, fwd_next, adj_now, adj_next)
+        )(src_index, *(pltpu.with_memory_space_constraint(value, pltpu.HBM) for value in arguments))
+        return pl.pallas_call(
+            functools.partial(update, shape),
+            out_shape=(
+                whole, jax.ShapeDtypeStruct(fwd_now.shape, f32), jax.ShapeDtypeStruct(adj_now.shape, f32)
+            ),
+            in_specs=[vmem] * 6,
+            out_specs=(hbm,) * 3,
+            scratch_shapes=[pltpu.VMEM(shape, f32), pltpu.VMEM(shape, f32), dma((7,))],
+            compiler_params=pltpu.CompilerParams(vmem_limit_bytes=8 * 1024 * 1024),
+            name="model_update",
+        )(*results)
 
     field = P(("groups", "shot"), "slab", None, None)
     model_spec = P(("groups", "slab"), None, None)

time: 105 us -> 98.1 us (0.934)
  local copies, waits for them, and re-layouts: 7.55 us -> 0 us
    unnamed x19 -> x0, local copies, waits for them, and re-layouts: 7.55 us -> none
where the time goes in v2:
time: 98.1 us; the launch traced here: 98 us
  Pallas kernels  96.7 us (99%)
  between operations  1.29 us (1%)
    pallas_call x1, Pallas kernels, per_device(): pl.pallas_call(functools.partial(kernel, shape, iters, shots, slabs), out...  95.7 us

profile of v2, /device:TPU:33, one launch (start us, length us, event | category | flops | bytes accessed | tf_op | source)
XLA Modules:
  0.0 98.0 jit_solution(4300029939352893237)
XLA Ops:
  1.3 95.7 %reverse_time.1 = (f32[8,64,128]{2,1,0:T(8,128)S(1)}, f32[8,128]{1,0:T(8,128)S(1)}, f32[8,64,128]{2,1,0:T(8,128)S(1)}, f32[8,64,128]{2,1,0:T(8,128)S(1)}, f32[8,...) custom-call(s32[1]{0:T(128)S(6)} %copy.12.src_index, f32[1,8]{1,0:T(1,128)} %wavelet_hbm.1, f32[1,8,128]{2,1,0:T(8,128)} %misfit_hbm.1, ...), custom_call_target="tpu_custom_call" | custom-call | tf_op jit(solution)/shard_map/reverse_time/pallas_call | solution.py:447
  97.0 1.0 model_update.1

commit v3 on v2

--- a/solution.py
+++ b/solution.py
@@ -17,9 +17,8 @@
     src_index, wavelet_hbm, misfit_hbm, rec_hbm, model_hbm, un_hbm, ul_hbm, an_hbm, al_hbm,
     grad_out, peak_out, model_out, base_out, lap_out, adjoint_out,
     now, mid, mod, lus, image, inj, src, onehot, misfit, rec, wavelet,
-    part, groups_sum, grad, peak_slab, peak_class,
-    load_sem, halo_send, halo_recv, first_send, first_recv, far_sem, near_sem,
-    rs_send, rs_recv, gs_send, gs_recv, relay_send, relay_recv, ag_send, ag_recv, ps_send, ps_recv, pc_send, pc_recv,
+    part, groups_sum, grad, tops,
+    load_sem, halo_send, halo_recv, far_sem, near_sem, sum_send, rs_recv, gs_recv, relay_recv, ag_recv, top_recv,
 ):
     depth, rows, cols = shape
     rounds = iters // 2
@@ -43,15 +42,18 @@
             src_ref=source, dst_ref=target, send_sem=send, recv_sem=recv, device_id=device, device_id_type=MESH
         )
 
+    def absorb(ref, sem):
+        pltpu.make_async_copy(ref, ref, sem).wait()
+
     loads = [
         pltpu.make_async_copy(un_hbm.at[0], now.at[0, 0, own, body], load_sem.at[0]),
+        pltpu.make_async_copy(ul_hbm.at[0], mid.at[0, 0, own, body], load_sem.at[0]),
+        pltpu.make_async_copy(model_hbm, mod.at[own], load_sem.at[0]),
         pltpu.make_async_copy(an_hbm.at[0], now.at[0, 1, own, body], load_sem.at[1]),
-        pltpu.make_async_copy(ul_hbm.at[0], mid.at[0, 0, own, body], load_sem.at[2]),
-        pltpu.make_async_copy(al_hbm.at[0], mid.at[0, 1, own, body], load_sem.at[3]),
-        pltpu.make_async_copy(model_hbm, mod.at[own], load_sem.at[4]),
-        pltpu.make_async_copy(misfit_hbm.at[0], misfit, load_sem.at[5]),
-        pltpu.make_async_copy(rec_hbm, rec, load_sem.at[6]),
-        pltpu.make_async_copy(wavelet_hbm, wavelet, load_sem.at[7]),
+        pltpu.make_async_copy(al_hbm.at[0], mid.at[0, 1, own, body], load_sem.at[1]),
+        pltpu.make_async_copy(misfit_hbm.at[0], misfit, load_sem.at[2]),
+        pltpu.make_async_copy(rec_hbm, rec, load_sem.at[3]),
+        pltpu.make_async_copy(wavelet_hbm, wavelet, load_sem.at[4]),
     ]
     for copy in loads:
         copy.start()
@@ -66,44 +68,27 @@
     def exists(side):
         return jnp.where(side == 0, slab > 0, slab < slabs - 1)
 
-    def halo(rnd, field, side):
-        return remote(
+    def send(side, source, target, rnd, field):
+        remote(
+            source, target, halo_send.at[side], halo_recv.at[rnd % 2, field, 1 - side], {"slab": slab + 2 * side - 1}
+        ).start()
+
+    def send_halo(rnd, field, side):
+        send(
+            side,
             now.at[rnd, field, pl.ds(2 + (depth - 2) * side, 2), body],
             now.at[rnd, field, pl.ds((depth + 2) * (1 - side), 2), body],
-            halo_send.at[rnd, field, side], halo_recv.at[rnd, field, 1 - side],
-            {"slab": slab + 2 * side - 1},
-        )
-
-    def halo_in(rnd, field, side):
-        return remote(
-            now.at[rnd, field, pl.ds(2 + (depth - 2) * side, 2), body],
-            now.at[rnd, field, pl.ds((depth + 2) * side, 2), body],
-            halo_send.at[rnd, field, side], halo_recv.at[rnd, field, side],
-            {"slab": slab + 2 * side - 1},
+            rnd, field,
         )
 
     def edge(side):
-        return 2 + (depth - 1) * side
+        return pl.ds(2 + (depth - 1) * side, 1)
 
     def ghost(side):
-        return 1 + (depth + 1) * side
-
-    def first_refs(which, plane):
-        if which == 2:
-            return mod.at[pl.ds(plane, 1)]
-        return mid.at[0, which, pl.ds(plane, 1), body]
-
-    def first(which, side, target, arrival):
-        return remote(
-            first_refs(which, edge(side)), first_refs(which, ghost(target)),
-            first_send.at[which, side], first_recv.at[which, arrival], {"slab": slab + 2 * side - 1},
-        )
-
-    def last(side, target, arrival):
-        return remote(
-            now.at[rounds, 0, pl.ds(edge(side), 1), body], now.at[rounds, 0, pl.ds(ghost(target), 1), body],
-            halo_send.at[rounds, 0, side], halo_recv.at[rounds, 0, arrival], {"slab": slab + 2 * side - 1},
-        )
+        return pl.ds(1 + (depth + 1) * side, 1)
+
+    def arrived(planes, rnd, field, side):
+        absorb(inj.at[0, pl.ds(0, planes)], halo_recv.at[rnd % 2, field, side])
 
     def on_sides(action):
         for side in sides:
@@ -111,20 +96,22 @@
             def _():
                 action(side)
 
-    loads[0].wait()
-    on_sides(lambda side: halo(0, 0, side).start())
-    loads[2].wait()
-    loads[4].wait()
-
-    def send_first_u(side):
-        first(0, side, 1 - side, 1 - side).start()
-        first(2, side, 1 - side, 1 - side).start()
-
-    on_sides(send_first_u)
-    loads[1].wait()
-    on_sides(lambda side: halo(0, 1, side).start())
-    loads[3].wait()
-    on_sides(lambda side: first(1, side, 1 - side, 1 - side).start())
+    def first_u(side):
+        send_halo(0, 0, side)
+        send(side, mid.at[0, 0, edge(side), body], mid.at[0, 0, ghost(1 - side), body], 0, 0)
+        send(side, mod.at[edge(side)], mod.at[ghost(1 - side)], 0, 0)
+
+    def first_a(side):
+        send_halo(0, 1, side)
+        send(side, mid.at[0, 1, edge(side), body], mid.at[0, 1, ghost(1 - side), body], 0, 1)
+
+    def last_u(side):
+        send(side, now.at[rounds, 0, edge(side), body], now.at[rounds, 0, ghost(1 - side), body], rounds, 0)
+
+    absorb(inj.at[0:2, 0 : depth + 4], load_sem.at[0])
+    on_sides(first_u)
+    absorb(inj.at[0:2, 0:depth], load_sem.at[1])
+    on_sides(first_a)
     for offset in (1, -1):
         signal(far_sem.at[0], at_shot(offset))
         signal(near_sem.at[0], at_slab(offset))
@@ -153,7 +140,7 @@
                     for rnd in range(rounds + 1):
                         now[rnd, field, at, body, :] = plane0
 
-    for copy in loads[5:]:
+    for copy in loads[-3:]:
         copy.wait()
     line = lax.shift_right_logical(rec[...], 7)
     lane = jnp.bitwise_and(rec[...], cols - 1)
@@ -228,60 +215,53 @@
     my_group = lax.div(me, WINDOW)
     count = shots // WINDOW
     half = depth // 2
-    sends = []
 
     def class_rows(which):
         return pl.ds(pl.multiple_of(which * height, height), height)
 
     def scatter(piece, source, length, target):
-        copies = []
         for slot, offset in enumerate(offsets):
             theirs = lax.rem(me + offset + shots, WINDOW)
-            copy = remote(
+            remote(
                 image.at[pl.ds(source, length), class_rows(theirs)], part.at[slot, pl.ds(target, length)],
-                rs_send.at[piece, slot], rs_recv.at[piece, slot], at_shot(offset),
-            )
-            copy.start()
-            copies.append(copy)
-        sends.extend(copies)
-        return copies
-
-    scattered = [[], []]
+                sum_send.at[0], rs_recv.at[piece], at_shot(offset),
+            ).start()
+
     for rnd in range(rounds):
         for field in range(2):
             both_steps(rnd, field, 3, depth - 2, 4, depth - 4)
         if rnd + 1 == rounds:
-            scattered[0] += scatter(0, 4, half, 0)
+            scatter(0, 4, half, 0)
         for side in sides:
             for field in range(2):
                 @pl.when(exists(side))
                 def _():
-                    halo_in(rnd, field, side).wait_recv()
                     if rnd == 0:
-                        first(field, side, side, side).wait_recv()
-                        if field == 0:
-                            first(2, side, side, side).wait_recv()
+                        arrived(4 - field, rnd, field, side)
+                    else:
+                        arrived(2, rnd, field, side)
 
                 both_steps(rnd, field, 1 + depth * side, 2, 2 + (depth - 2) * side, 2)
 
                 if rnd + 1 == rounds and field == 1:
-                    scattered[1] += scatter(1 + side, 2 + (depth - 2) * side, 2, half + 2 * side)
+                    scatter(1, 2 + (depth - 2) * side, 2, half + 2 * side)
 
                 @pl.when(exists(side))
                 def _():
                     if rnd + 1 < rounds:
-                        halo(rnd + 1, field, side).start()
+                        send_halo(rnd + 1, field, side)
                     elif field == 0:
-                        last(side, 1 - side, 1 - side).start()
-        if rnd < 3:
-            pl.semaphore_wait(far_sem.at[rnd], 2)
-        if rnd < 2:
-            for offset in (2 << rnd, -(2 << rnd)):
-                signal(far_sem.at[rnd + 1], at_shot(offset))
-            pl.semaphore_wait(near_sem.at[rnd], 2)
+                        last_u(side)
         if rnd == 0:
+            pl.semaphore_wait(near_sem.at[0], 2)
             for offset in (2, -2):
                 signal(near_sem.at[1], at_slab(offset))
+        elif rnd == 1:
+            pl.semaphore_wait(near_sem.at[1], 2)
+        if 0 < rnd < 3:
+            pl.semaphore_wait(far_sem.at[rnd - 1], 2)
+            for offset in (1 << rnd, -(1 << rnd)):
+                signal(far_sem.at[rnd], at_shot(offset))
 
     def at_group(turn):
         return lax.rem(my_group + turn + count, count)
@@ -290,7 +270,7 @@
         start = half * piece
         mine = groups_sum.at[my_group, pl.ds(start, half)]
         return remote(
-            mine, mine, gs_send.at[piece, turn], gs_recv.at[piece, turn], at_shot(WINDOW if turn else -WINDOW)
+            mine, mine, sum_send.at[1], gs_recv.at[piece, turn], at_shot(WINDOW if turn else -WINDOW)
         )
 
     def passed_in(piece, turn):
@@ -298,31 +278,30 @@
         origin = at_group(-1 if turn else 1)
         theirs = groups_sum.at[origin, pl.ds(start, half)]
         return remote(
-            theirs, theirs, gs_send.at[piece, turn], gs_recv.at[piece, turn], at_shot(WINDOW if turn else -WINDOW)
+            theirs, theirs, sum_send.at[1], gs_recv.at[piece, turn], at_shot(WINDOW if turn else -WINDOW)
         )
 
     def relayed(piece, turn, origin):
         start = half * piece + (half // 2) * (1 - turn)
         theirs = groups_sum.at[origin, pl.ds(start, half // 2)]
         return remote(
-            theirs, theirs, relay_send.at[piece, turn], relay_recv.at[piece, turn], at_shot(WINDOW if turn else -WINDOW)
+            theirs, theirs, sum_send.at[1], relay_recv.at[piece, turn], at_shot(WINDOW if turn else -WINDOW)
         )
 
     for piece in range(2):
-        for copy in scattered[piece]:
-            copy.wait_recv()
+        absorb(part.at[:, pl.ds(half * piece, half)], rs_recv.at[piece])
         for slot in range(half * piece, half * (piece + 1)):
             plane = slot + 4 if piece == 0 else (slot - half + 2 if slot < half + 2 else slot + 2)
             total = image[plane, class_rows(my_class), :]
             for index in range(len(offsets)):
                 total = total + part[index, slot]
             groups_sum[my_group, slot] = total
+        if piece == 0:
+            pl.semaphore_wait(far_sem.at[2], 2)
         for turn in range(2):
-            copy = passed(piece, turn)
-            copy.start()
-            sends.append(copy)
-
-    on_sides(lambda side: last(side, side, side).wait_recv())
+            passed(piece, turn).start()
+
+    on_sides(lambda side: arrived(1, rounds, 0, side))
 
     def prepare(plane, carry):
         state = now.at[rounds, 0]
@@ -337,9 +316,7 @@
     for piece in range(2):
         for turn in range(2):
             passed_in(piece, turn).wait_recv()
-            copy = relayed(piece, turn, at_group(-1 if turn else 1))
-            copy.start()
-            sends.append(copy)
+            relayed(piece, turn, at_group(-1 if turn else 1)).start()
 
     top = jnp.zeros((height, cols), jnp.float32)
     for piece in range(2):
@@ -352,53 +329,41 @@
             grad[slot, class_rows(my_class), :] = total
             top = jnp.maximum(top, jnp.abs(total))
         if piece == 1:
-            peak_slab[slab] = top
-            for turn in range(1, slabs):
-                copy = remote(peak_slab.at[slab], peak_slab.at[slab], ps_send.at[turn], ps_recv.at[turn], at_slab(turn))
-                copy.start()
-                sends.append(copy)
-        for slot, offset in enumerate(offsets):
+            mark_top = tops.at[pl.ds(my_class * slabs + slab, 1)]
+            tops[my_class * slabs + slab] = jnp.max(top, axis=0, keepdims=True)
+
+            def tell(turn, carry):
+                for offset in offsets:
+                    remote(
+                        mark_top, mark_top, sum_send.at[3], top_recv.at[0], {**at_shot(offset), **at_slab(turn)}
+                    ).start()
+                return carry
+
+            def tell_here(turn, carry):
+                remote(mark_top, mark_top, sum_send.at[3], top_recv.at[0], at_slab(turn)).start()
+                return carry
+
+            lax.fori_loop(0, slabs, tell, 0)
+            lax.fori_loop(1, slabs, tell_here, 0)
+        for offset in offsets:
             mine = grad.at[pl.ds(half * piece, half), class_rows(my_class)]
-            copy = remote(mine, mine, ag_send.at[piece, slot], ag_recv.at[piece, slot], at_shot(offset))
-            copy.start()
-            sends.append(copy)
-    for turn in range(1, slabs):
-        theirs = peak_slab.at[lax.rem(slab + slabs - turn, slabs)]
-        remote(theirs, theirs, ps_send.at[turn], ps_recv.at[turn], at_slab(turn)).wait_recv()
-    top = peak_slab[0]
-    for other in range(1, slabs):
-        top = jnp.maximum(top, peak_slab[other])
-    peak_class[my_class] = top
-    for slot, offset in enumerate(offsets):
-        mine = peak_class.at[my_class]
-        copy = remote(mine, mine, pc_send.at[slot], pc_recv.at[slot], at_shot(offset))
-        copy.start()
-        sends.append(copy)
+            remote(mine, mine, sum_send.at[2], ag_recv.at[piece], at_shot(offset)).start()
     for piece in range(2):
-        for slot, offset in enumerate(offsets):
-            theirs = grad.at[pl.ds(half * piece, half), class_rows(lax.rem(me - offset + shots, WINDOW))]
-            remote(theirs, theirs, ag_send.at[piece, slot], ag_recv.at[piece, slot], at_shot(offset)).wait_recv()
+        absorb(part.at[:, pl.ds(half * piece, half)], ag_recv.at[piece])
         for slot in range(half * piece, half * (piece + 1)):
             grad_out[slot] = grad[slot]
-    for slot, offset in enumerate(offsets):
-        theirs = peak_class.at[lax.rem(me - offset + shots, WINDOW)]
-        remote(theirs, theirs, pc_send.at[slot], pc_recv.at[slot], at_shot(offset)).wait_recv()
-    top = peak_class[0]
-    for other in range(1, WINDOW):
-        top = jnp.maximum(top, peak_class[other])
+    others = tops.at[pl.ds(0, WINDOW * slabs - 1)]
+    absorb(others, top_recv.at[0])
+    top = tops[0]
+    for other in range(1, WINDOW * slabs):
+        top = jnp.maximum(top, tops[other])
     peak_out[...] = top
 
-    def sent(side):
-        for field in range(2):
-            for rnd in range(rounds):
-                halo(rnd, field, side).wait_send()
-        last(side, 1 - side, 1 - side).wait_send()
-        for which in range(3):
-            first(which, side, 1 - side, 1 - side).wait_send()
-
-    on_sides(sent)
-    for copy in sends:
-        copy.wait_send()
+    on_sides(lambda side: absorb(inj.at[0:2, 0 : 2 * rounds + 2], halo_send.at[side]))
+    absorb(part, sum_send.at[0])
+    absorb(groups_sum.at[pl.ds(0, count - 1)], sum_send.at[1])
+    absorb(part, sum_send.at[2])
+    absorb(others, sum_send.at[3])
 
 
 def update(shape, grad, top, model, base, lap, adjoint, new_model_hbm, stepped_hbm, adjoint_hbm, fresh_all, step_all, sem):
@@ -406,7 +371,7 @@
     half = depth // 2
     kept = pltpu.make_async_copy(adjoint, adjoint_hbm.at[0], sem.at[0])
     kept.start()
-    peak = jnp.max(jnp.max(top[...], axis=0, keepdims=True), axis=1, keepdims=True) + 1e-6
+    peak = jnp.max(top[...], axis=1, keepdims=True) + 1e-6
     copies = [kept]
     for slot in range(depth):
         plane = slot + 2 if slot < half else (slot - half if slot < half + 2 else slot)
@@ -446,7 +411,7 @@
         arguments = (wavelet, misfit, rec_index, model, fwd_now, fwd_next, adj_now, adj_next)
         results = pl.pallas_call(
             functools.partial(kernel, shape, iters, shots, slabs),
-            out_shape=(whole, jax.ShapeDtypeStruct((height, cols), f32), whole, whole, whole, whole),
+            out_shape=(whole, jax.ShapeDtypeStruct((1, cols), f32), whole, whole, whole, whole),
             in_specs=[pl.BlockSpec(memory_space=pltpu.SMEM)] + [hbm] * 8,
             out_specs=(vmem,) * 6,
             scratch_shapes=[
@@ -464,18 +429,18 @@
                 pltpu.VMEM((WINDOW - 1, depth, height, cols), f32),
                 pltpu.VMEM((shots // WINDOW, depth, height, cols), f32),
                 pltpu.VMEM(shape, f32),
-                pltpu.VMEM((slabs, height, cols), f32),
-                pltpu.VMEM((WINDOW, height, cols), f32),
-                dma((8,)),
-                dma((rounds + 1, 2, 2)), dma((rounds + 1, 2, 2)),
-                dma((3, 2)), dma((3, 2)),
-                pltpu.SemaphoreType.REGULAR((3,)), pltpu.SemaphoreType.REGULAR((2,)),
-                dma((3, WINDOW - 1)), dma((3, WINDOW - 1)),
-                dma((2, 2)), dma((2, 2)),
-                dma((2, 2)), dma((2, 2)),
-                dma((2, WINDOW - 1)), dma((2, WINDOW - 1)),
-                dma((slabs,)), dma((slabs,)),
-                dma((WINDOW - 1,)), dma((WINDOW - 1,)),
+                pltpu.VMEM((WINDOW * slabs, 1, cols), f32),
+                dma((5,)),
+                dma((2,)),
+                dma((2, 2, 2)),
+                pltpu.SemaphoreType.REGULAR((3,)),
+                pltpu.SemaphoreType.REGULAR((2,)),
+                dma((4,)),
+                dma((2,)),
+                dma((2, 2)),
+                dma((2, 2)),
+                dma((2,)),
+                dma((1,)),
             ],
             compiler_params=pltpu.CompilerParams(
                 collective_id=0, has_side_effects=True, vmem_limit_bytes=48 * 1024 * 1024

time: 98.1 us -> 96.3 us (0.982)
  Pallas kernels: 96.7 us -> 94.9 us
    pallas_call x1, Pallas kernels: 95.7 us -> 93.9 us  [per_device(): pl.pallas_call(functools.partial(kernel, shape, iters, shots, slabs), out...]
where the time goes in v3:
time: 96.3 us; the launch traced here: 96.2 us
  Pallas kernels  94.9 us (99%)
  between operations  1.29 us (1%)
    pallas_call x1, Pallas kernels, per_device(): pl.pallas_call(functools.partial(kernel, shape, iters, shots, slabs), out...  93.9 us

profile of v3, /device:TPU:33, one launch (start us, length us, event | category | flops | bytes accessed | tf_op | source)
XLA Modules:
  0.0 96.2 jit_solution(231326707381682083)
XLA Ops:
  1.3 93.9 %reverse_time.1 = (f32[8,64,128]{2,1,0:T(8,128)S(1)}, f32[1,128]{1,0:T(1,128)S(1)}, f32[8,64,128]{2,1,0:T(8,128)S(1)}, f32[8,64,128]{2,1,0:T(8,128)S(1)}, f32[8,...) custom-call(s32[1]{0:T(128)S(6)} %copy.12.src_index, f32[1,8]{1,0:T(1,128)} %wavelet_hbm.1, f32[1,8,128]{2,1,0:T(8,128)} %misfit_hbm.1, ...), custom_call_target="tpu_custom_call" | custom-call | tf_op jit(solution)/shard_map/reverse_time/pallas_call | solution.py:412
  95.2 1.0 model_update.1

commit v4 on v3

--- a/solution.py
+++ b/solution.py
@@ -119,16 +119,17 @@
     strip = jnp.zeros((PAD, cols), jnp.float32)
     plane0 = jnp.zeros((rows, cols), jnp.float32)
 
-    def clear(plane, carry):
-        for rnd in range(rounds + 1):
-            for field in range(2):
-                for ref in (now, mid):
-                    ref[rnd, field, plane, 0:PAD, :] = strip
-                    ref[rnd, field, plane, PAD + rows : PAD + rows + PAD, :] = strip
-        image[plane] = plane0
-        return carry
-
-    lax.fori_loop(0, depth + 4, clear, 0)
+    def borders(*refs):
+        def clear(plane, carry):
+            for ref in refs:
+                for field in range(2):
+                    ref[field, plane, 0:PAD, :] = strip
+                    ref[field, plane, PAD + rows : PAD + rows + PAD, :] = strip
+            return carry
+
+        lax.fori_loop(0, depth + 4, clear, 0)
+
+    borders(now.at[0], mid.at[1])
     for side in range(2):
         @pl.when(jnp.logical_not(exists(side)))
         def _():
@@ -155,6 +156,7 @@
         at = pl.ds(pl.multiple_of(plane * rows, rows), rows)
         for copy in range(3):
             onehot[at, copy * cols : (copy + 1) * cols] = hit
+        image[plane] = plane0
         src[plane] = jnp.where((here == src_line) & (col_id == src_lane), 1.0, 0.0)
         return carry
 
@@ -174,7 +176,7 @@
         inj[k, 1 : depth + 3] = added.reshape(depth + 2, rows, cols)
         return carry
 
-    lax.fori_loop(0, iters, place, 0)
+    lax.fori_loop(0, 2, place, 0)
 
     first_lane = col_id == 0
     last_lane = col_id == cols - 1
@@ -232,7 +234,10 @@
             both_steps(rnd, field, 3, depth - 2, 4, depth - 4)
         if rnd + 1 == rounds:
             scatter(0, 4, half, 0)
-        for side in sides:
+        for turn, side in enumerate(sides):
+            if turn == 1 and rnd + 1 < rounds:
+                borders(now.at[rnd + 1], mid.at[rnd + 2])
+                lax.fori_loop(2 * rnd + 2, 2 * rnd + 4, place, 0)
             for field in range(2):
                 @pl.when(exists(side))
                 def _():
@@ -274,18 +279,15 @@
         )
 
     def passed_in(piece, turn):
-        start = half * piece
-        origin = at_group(-1 if turn else 1)
-        theirs = groups_sum.at[origin, pl.ds(start, half)]
+        theirs = groups_sum.at[at_group(1 - 2 * turn), pl.ds(half * piece, half)]
         return remote(
-            theirs, theirs, sum_send.at[1], gs_recv.at[piece, turn], at_shot(WINDOW if turn else -WINDOW)
+            theirs, theirs, sum_send.at[1], gs_recv.at[piece, turn], at_shot((2 * turn - 1) * WINDOW)
         )
 
     def relayed(piece, turn, origin):
-        start = half * piece + (half // 2) * (1 - turn)
-        theirs = groups_sum.at[origin, pl.ds(start, half // 2)]
+        theirs = groups_sum.at[origin, pl.ds(half * piece + (half // 2) * (1 - turn), half // 2)]
         return remote(
-            theirs, theirs, sum_send.at[1], relay_recv.at[piece, turn], at_shot(WINDOW if turn else -WINDOW)
+            theirs, theirs, sum_send.at[1], relay_recv.at[piece, turn], at_shot((2 * turn - 1) * WINDOW)
         )
 
     for piece in range(2):
@@ -312,11 +314,13 @@
         model_out[plane - 2] = mod[plane]
         return carry
 
+    borders(now.at[rounds])
     lax.fori_loop(2, depth + 2, prepare, 0)
-    for piece in range(2):
-        for turn in range(2):
+    early = jnp.where(at_group(-1) < at_group(1), 1, 0)
+    for number, turn in enumerate((early, 1 - early)):
+        for piece in range(2):
             passed_in(piece, turn).wait_recv()
-            relayed(piece, turn, at_group(-1 if turn else 1)).start()
+            relayed(piece, turn, at_group(1 - 2 * turn)).start()
 
     top = jnp.zeros((height, cols), jnp.float32)
     for piece in range(2):

time: 96.3 us -> 95.1 us (0.988)
  Pallas kernels: 94.9 us -> 93.7 us
    pallas_call x1, Pallas kernels: 93.9 us -> 92.7 us  [per_device(): pl.pallas_call(functools.partial(kernel, shape, iters, shots, slabs), out...]
where the time goes in v4:
time: 95.1 us; the launch traced here: 95 us
  Pallas kernels  93.7 us (99%)
  between operations  1.29 us (1%)
    pallas_call x1, Pallas kernels, per_device(): pl.pallas_call(functools.partial(kernel, shape, iters, shots, slabs), out...  92.7 us

profile of v4, /device:TPU:33, one launch (start us, length us, event | category | flops | bytes accessed | tf_op | source)
XLA Modules:
  0.0 95.0 jit_solution(8565357689510181456)
XLA Ops:
  1.3 92.7 %reverse_time.1 = (f32[8,64,128]{2,1,0:T(8,128)S(1)}, f32[1,128]{1,0:T(1,128)S(1)}, f32[8,64,128]{2,1,0:T(8,128)S(1)}, f32[8,64,128]{2,1,0:T(8,128)S(1)}, f32[8,...) custom-call(s32[1]{0:T(128)S(6)} %copy.12.src_index, f32[1,8]{1,0:T(1,128)} %wavelet_hbm.1, f32[1,8,128]{2,1,0:T(8,128)} %misfit_hbm.1, ...), custom_call_target="tpu_custom_call" | custom-call | tf_op jit(solution)/shard_map/reverse_time/pallas_call | solution.py:416
  94.0 1.0 %model_update.1 = (f32[8,64,128]{2,1,0:T(8,128)}, f32[1,8,64,128]{3,2,1,0:T(8,128)}, f32[1,8,64,128]{3,2,1,0:T(8,128)}) custom-call(f32[8,64,128]{2,1,0:T(8,128)S(1)} %get-tuple-element.9.grad, f32[1,128]{1,0:T(1,128)S(1)} %get-tuple-element.10.top, f32[8,64,128]{2,1,0:T(8,128)S(1)} %get-tuple-element.11.model, f32[8,64,128]{2,1,0:T(8,128)S(1)} %get-tuple-element.12.base, ...), custom_call_target="tpu_custom_call" | custom-call | tf_op jit(solution)/shard_map/model_update/pallas_call | solution.py:454

commit v5 on v4

--- a/solution.py
+++ b/solution.py
@@ -160,7 +160,7 @@
         src[plane] = jnp.where((here == src_line) & (col_id == src_lane), 1.0, 0.0)
         return carry
 
-    lax.fori_loop(1, depth + 3, mark, 0)
+    lax.fori_loop(1, depth + 3, mark, 0, unroll=2)
     cell_id = lax.broadcasted_iota(jnp.int32, (cols, cols), 0)
 
     def place(k, carry):
@@ -176,7 +176,7 @@
         inj[k, 1 : depth + 3] = added.reshape(depth + 2, rows, cols)
         return carry
 
-    lax.fori_loop(0, 2, place, 0)
+    lax.fori_loop(0, 2, place, 0, unroll=True)
 
     first_lane = col_id == 0
     last_lane = col_id == cols - 1
@@ -189,7 +189,7 @@
         return beside + (left + right) - 6.0 * center
 
     def advance(field, state, later, target, start, count, k, slot):
-        def one(index, carry):
+        def one(index):
             plane = start + index
             center = state[plane, body, :]
             lap = laplace(state, plane, center)
@@ -201,9 +201,9 @@
                 image[plane] = image[plane] + center * lus[slot, plane]
                 fresh = fresh + inj[k, plane]
             target[plane, body, :] = fresh
-            return carry
-
-        lax.fori_loop(0, count, one, 0)
+
+        for index in range(count):
+            one(index)
 
     def both_steps(rnd, field, first_at, first_count, second_at, second_count):
         a, b, c, d = now.at[rnd, field], mid.at[rnd, field], mid.at[rnd + 1, field], now.at[rnd + 1, field]
@@ -237,7 +237,7 @@
         for turn, side in enumerate(sides):
             if turn == 1 and rnd + 1 < rounds:
                 borders(now.at[rnd + 1], mid.at[rnd + 2])
-                lax.fori_loop(2 * rnd + 2, 2 * rnd + 4, place, 0)
+                lax.fori_loop(2 * rnd + 2, 2 * rnd + 4, place, 0, unroll=True)
             for field in range(2):
                 @pl.when(exists(side))
                 def _():
@@ -315,7 +315,7 @@
         return carry
 
     borders(now.at[rounds])
-    lax.fori_loop(2, depth + 2, prepare, 0)
+    lax.fori_loop(2, depth + 2, prepare, 0, unroll=4)
     early = jnp.where(at_group(-1) < at_group(1), 1, 0)
     for number, turn in enumerate((early, 1 - early)):
         for piece in range(2):

time: 95.1 us -> 91.1 us (0.958)
  Pallas kernels: 93.7 us -> 89.6 us
    pallas_call x1, Pallas kernels: 92.7 us -> 88.7 us  [per_device(): pl.pallas_call(functools.partial(kernel, shape, iters, shots, slabs), out...]
where the time goes in v5:
time: 91.1 us; the launch traced here: 90.9 us
  Pallas kernels  89.6 us (98%)
  between operations  1.29 us (1%)
    pallas_call x1, Pallas kernels, per_device(): pl.pallas_call(functools.partial(kernel, shape, iters, shots, slabs), out...  88.7 us

profile of v5, /device:TPU:33, one launch (start us, length us, event | category | flops | bytes accessed | tf_op | source)
XLA Modules:
  0.0 90.9 jit_solution(5982139828591409049)
XLA Ops:
  1.3 88.7 %reverse_time.1 = (f32[8,64,128]{2,1,0:T(8,128)S(1)}, f32[1,128]{1,0:T(1,128)S(1)}, f32[8,64,128]{2,1,0:T(8,128)S(1)}, f32[8,64,128]{2,1,0:T(8,128)S(1)}, f32[8,...) custom-call(s32[1]{0:T(128)S(6)} %copy.12.src_index, f32[1,8]{1,0:T(1,128)} %wavelet_hbm.1, f32[1,8,128]{2,1,0:T(8,128)} %misfit_hbm.1, ...), custom_call_target="tpu_custom_call" | custom-call | tf_op jit(solution)/shard_map/reverse_time/pallas_call | solution.py:416
  90.0 1.0 %model_update.1 = (f32[8,64,128]{2,1,0:T(8,128)}, f32[1,8,64,128]{3,2,1,0:T(8,128)}, f32[1,8,64,128]{3,2,1,0:T(8,128)}) custom-call(f32[8,64,128]{2,1,0:T(8,128)S(1)} %get-tuple-element.9.grad, f32[1,128]{1,0:T(1,128)S(1)} %get-tuple-element.10.top, f32[8,64,128]{2,1,0:T(8,128)S(1)} %get-tuple-element.11.model, f32[8,64,128]{2,1,0:T(8,128)S(1)} %get-tuple-element.12.base, ...), custom_call_target="tpu_custom_call" | custom-call | tf_op jit(solution)/shard_map/model_update/pallas_call | solution.py:454

commit v6 on v5

--- a/solution.py
+++ b/solution.py
@@ -217,15 +217,20 @@
     my_group = lax.div(me, WINDOW)
     count = shots // WINDOW
     half = depth // 2
+    pieces = ((0, half, 2), (half, 2, (depth - 2) * sides[0]), (half + 2, 2, (depth - 2) * sides[1]))
+
+    def slots(piece):
+        return pl.ds(*pieces[piece][:2])
 
     def class_rows(which):
         return pl.ds(pl.multiple_of(which * height, height), height)
 
-    def scatter(piece, source, length, target):
+    def scatter(piece):
+        start, length, plane = pieces[piece]
         for slot, offset in enumerate(offsets):
             theirs = lax.rem(me + offset + shots, WINDOW)
             remote(
-                image.at[pl.ds(source, length), class_rows(theirs)], part.at[slot, pl.ds(target, length)],
+                image.at[pl.ds(plane + 2, length), class_rows(theirs)], part.at[slot, pl.ds(start, length)],
                 sum_send.at[0], rs_recv.at[piece], at_shot(offset),
             ).start()
 
@@ -233,7 +238,7 @@
         for field in range(2):
             both_steps(rnd, field, 3, depth - 2, 4, depth - 4)
         if rnd + 1 == rounds:
-            scatter(0, 4, half, 0)
+            scatter(0)
         for turn, side in enumerate(sides):
             if turn == 1 and rnd + 1 < rounds:
                 borders(now.at[rnd + 1], mid.at[rnd + 2])
@@ -249,7 +254,7 @@
                 both_steps(rnd, field, 1 + depth * side, 2, 2 + (depth - 2) * side, 2)
 
                 if rnd + 1 == rounds and field == 1:
-                    scatter(1, 2 + (depth - 2) * side, 2, half + 2 * side)
+                    scatter(1 + turn)
 
                 @pl.when(exists(side))
                 def _():
@@ -272,32 +277,31 @@
         return lax.rem(my_group + turn + count, count)
 
     def passed(piece, turn):
-        start = half * piece
-        mine = groups_sum.at[my_group, pl.ds(start, half)]
+        mine = groups_sum.at[my_group, slots(piece)]
         return remote(
             mine, mine, sum_send.at[1], gs_recv.at[piece, turn], at_shot(WINDOW if turn else -WINDOW)
         )
 
     def passed_in(piece, turn):
-        theirs = groups_sum.at[at_group(1 - 2 * turn), pl.ds(half * piece, half)]
+        theirs = groups_sum.at[at_group(1 - 2 * turn), slots(piece)]
         return remote(
             theirs, theirs, sum_send.at[1], gs_recv.at[piece, turn], at_shot((2 * turn - 1) * WINDOW)
         )
 
     def relayed(piece, turn, origin):
-        theirs = groups_sum.at[origin, pl.ds(half * piece + (half // 2) * (1 - turn), half // 2)]
+        start, length, _ = pieces[piece]
+        theirs = groups_sum.at[origin, pl.ds(start + (length // 2) * (1 - turn), length // 2)]
         return remote(
             theirs, theirs, sum_send.at[1], relay_recv.at[piece, turn], at_shot((2 * turn - 1) * WINDOW)
         )
 
-    for piece in range(2):
-        absorb(part.at[:, pl.ds(half * piece, half)], rs_recv.at[piece])
-        for slot in range(half * piece, half * (piece + 1)):
-            plane = slot + 4 if piece == 0 else (slot - half + 2 if slot < half + 2 else slot + 2)
-            total = image[plane, class_rows(my_class), :]
-            for index in range(len(offsets)):
-                total = total + part[index, slot]
-            groups_sum[my_group, slot] = total
+    for piece, (start, length, plane) in enumerate(pieces):
+        absorb(part.at[:, slots(piece)], rs_recv.at[piece])
+        for index in range(length):
+            total = image[plane + 2 + index, class_rows(my_class), :]
+            for other in range(len(offsets)):
+                total = total + part[other, start + index]
+            groups_sum[my_group, start + index] = total
         if piece == 0:
             pl.semaphore_wait(far_sem.at[2], 2)
         for turn in range(2):
@@ -318,44 +322,47 @@
     lax.fori_loop(2, depth + 2, prepare, 0, unroll=4)
     early = jnp.where(at_group(-1) < at_group(1), 1, 0)
     for number, turn in enumerate((early, 1 - early)):
-        for piece in range(2):
+        for piece in range(len(pieces)):
             passed_in(piece, turn).wait_recv()
             relayed(piece, turn, at_group(1 - 2 * turn)).start()
 
+    mark_top = tops.at[pl.ds(my_class * slabs + slab, 1)]
+
+    def tell(offset, first_slab):
+        def one(turn, carry):
+            where = {**at_shot(offset), **at_slab(turn)} if first_slab == 0 else at_slab(turn)
+            remote(mark_top, mark_top, sum_send.at[3], top_recv.at[0], where).start()
+            return carry
+
+        lax.fori_loop(first_slab, slabs, one, 0)
+
+    def share(piece):
+        for offset in offsets:
+            mine = grad.at[slots(piece), class_rows(my_class)]
+            remote(mine, mine, sum_send.at[2], ag_recv.at[piece], at_shot(offset)).start()
+
     top = jnp.zeros((height, cols), jnp.float32)
-    for piece in range(2):
+    for piece, (start, length, plane) in enumerate(pieces):
         for turn in range(2):
             relayed(piece, turn, at_group(2)).wait_recv()
-        for slot in range(half * piece, half * (piece + 1)):
+        for slot in range(start, start + length):
             total = groups_sum[0, slot]
             for group in range(1, count):
                 total = total + groups_sum[group, slot]
             grad[slot, class_rows(my_class), :] = total
             top = jnp.maximum(top, jnp.abs(total))
-        if piece == 1:
-            mark_top = tops.at[pl.ds(my_class * slabs + slab, 1)]
-            tops[my_class * slabs + slab] = jnp.max(top, axis=0, keepdims=True)
-
-            def tell(turn, carry):
-                for offset in offsets:
-                    remote(
-                        mark_top, mark_top, sum_send.at[3], top_recv.at[0], {**at_shot(offset), **at_slab(turn)}
-                    ).start()
-                return carry
-
-            def tell_here(turn, carry):
-                remote(mark_top, mark_top, sum_send.at[3], top_recv.at[0], at_slab(turn)).start()
-                return carry
-
-            lax.fori_loop(0, slabs, tell, 0)
-            lax.fori_loop(1, slabs, tell_here, 0)
-        for offset in offsets:
-            mine = grad.at[pl.ds(half * piece, half), class_rows(my_class)]
-            remote(mine, mine, sum_send.at[2], ag_recv.at[piece], at_shot(offset)).start()
-    for piece in range(2):
-        absorb(part.at[:, pl.ds(half * piece, half)], ag_recv.at[piece])
-        for slot in range(half * piece, half * (piece + 1)):
-            grad_out[slot] = grad[slot]
+        if piece + 1 < len(pieces):
+            share(piece)
+    tops[my_class * slabs + slab] = jnp.max(top, axis=0, keepdims=True)
+    for number, offset in enumerate(offsets):
+        tell(offset, 0)
+        if number == 2:
+            share(len(pieces) - 1)
+    tell(0, 1)
+    for piece, (start, length, plane) in enumerate(pieces):
+        absorb(part.at[:, slots(piece)], ag_recv.at[piece])
+        for index in range(length):
+            grad_out[plane + index] = grad[start + index]
     others = tops.at[pl.ds(0, WINDOW * slabs - 1)]
     absorb(others, top_recv.at[0])
     top = tops[0]
@@ -377,23 +384,16 @@
     kept.start()
     peak = jnp.max(top[...], axis=1, keepdims=True) + 1e-6
     copies = [kept]
-    for slot in range(depth):
-        plane = slot + 2 if slot < half else (slot - half if slot < half + 2 else slot)
-        fresh = jnp.clip(model[plane] - 0.1 * grad[slot] / peak, 0.05, 0.3)
+    for plane in range(depth):
+        fresh = jnp.clip(model[plane] - 0.1 * grad[plane] / peak, 0.05, 0.3)
         fresh_all[plane] = fresh
         step_all[plane] = base[plane] + fresh * lap[plane]
-        if slot == half - 1:
-            planes = pl.ds(2, half)
-        elif slot == half + 1:
-            planes = pl.ds(0, 2)
-        elif slot == depth - 1:
-            planes = pl.ds(depth - 2, 2)
-        else:
-            continue
-        for source, target in ((fresh_all, new_model_hbm), (step_all, stepped_hbm.at[0])):
-            copy = pltpu.make_async_copy(source.at[planes], target.at[planes], sem.at[len(copies)])
-            copy.start()
-            copies.append(copy)
+        if (plane + 1) % half == 0:
+            planes = pl.ds(plane + 1 - half, half)
+            for source, target in ((fresh_all, new_model_hbm), (step_all, stepped_hbm.at[0])):
+                copy = pltpu.make_async_copy(source.at[planes], target.at[planes], sem.at[len(copies)])
+                copy.start()
+                copies.append(copy)
     for copy in copies:
         copy.wait()
 
@@ -440,10 +440,10 @@
                 pltpu.SemaphoreType.REGULAR((3,)),
                 pltpu.SemaphoreType.REGULAR((2,)),
                 dma((4,)),
-                dma((2,)),
-                dma((2, 2)),
-                dma((2, 2)),
-                dma((2,)),
+                dma((3,)),
+                dma((3, 2)),
+                dma((3, 2)),
+                dma((3,)),
                 dma((1,)),
             ],
             compiler_params=pltpu.CompilerParams(
@@ -458,7 +458,7 @@
             ),
             in_specs=[vmem] * 6,
             out_specs=(hbm,) * 3,
-            scratch_shapes=[pltpu.VMEM(shape, f32), pltpu.VMEM(shape, f32), dma((7,))],
+            scratch_shapes=[pltpu.VMEM(shape, f32), pltpu.VMEM(shape, f32), dma((5,))],
             compiler_params=pltpu.CompilerParams(vmem_limit_bytes=8 * 1024 * 1024),
             name="model_update",
         )(*results)

time: 91.1 us -> 91.7 us (level)
  no operation moved by 1% of the time
where the time goes in v6:
time: 91.7 us; the launch traced here: 91.5 us
  Pallas kernels  90.3 us (98%)
  between operations  1.29 us (1%)
    pallas_call x1, Pallas kernels, per_device(): pl.pallas_call(functools.partial(kernel, shape, iters, shots, slabs), out...  89.3 us

profile of v6, /device:TPU:33, one launch (start us, length us, event | category | flops | bytes accessed | tf_op | source)
XLA Modules:
  0.0 91.5 jit_solution(418484777950043810)
XLA Ops:
  1.3 89.3 %reverse_time.1 = (f32[8,64,128]{2,1,0:T(8,128)S(1)}, f32[1,128]{1,0:T(1,128)S(1)}, f32[8,64,128]{2,1,0:T(8,128)S(1)}, f32[8,64,128]{2,1,0:T(8,128)S(1)}, f32[8,...) custom-call(s32[1]{0:T(128)S(6)} %copy.12.src_index, f32[1,8]{1,0:T(1,128)} %wavelet_hbm.1, f32[1,8,128]{2,1,0:T(8,128)} %misfit_hbm.1, ...), custom_call_target="tpu_custom_call" | custom-call | tf_op jit(solution)/shard_map/reverse_time/pallas_call | solution.py:416
  90.6 0.9 %model_update.1 = (f32[8,64,128]{2,1,0:T(8,128)}, f32[1,8,64,128]{3,2,1,0:T(8,128)}, f32[1,8,64,128]{3,2,1,0:T(8,128)}) custom-call(f32[8,64,128]{2,1,0:T(8,128)S(1)} %get-tuple-element.9.grad, f32[1,128]{1,0:T(1,128)S(1)} %get-tuple-element.10.top, f32[8,64,128]{2,1,0:T(8,128)S(1)} %get-tuple-element.11.model, f32[8,64,128]{2,1,0:T(8,128)S(1)} %get-tuple-element.12.base, ...), custom_call_target="tpu_custom_call" | custom-call | tf_op jit(solution)/shard_map/model_update/pallas_call | solution.py:454

commit v7 on v6

--- a/solution.py
+++ b/solution.py
@@ -217,7 +217,8 @@
     my_group = lax.div(me, WINDOW)
     count = shots // WINDOW
     half = depth // 2
-    pieces = ((0, half, 2), (half, 2, (depth - 2) * sides[0]), (half + 2, 2, (depth - 2) * sides[1]))
+    pieces = [(0, half, 2)]
+    pieces += [(half + 2 * turn, 2, (depth - 2) * side) for turn, side in enumerate(sides)]
 
     def slots(piece):
         return pl.ds(*pieces[piece][:2])
@@ -328,13 +329,11 @@
 
     mark_top = tops.at[pl.ds(my_class * slabs + slab, 1)]
 
-    def tell(offset, first_slab):
-        def one(turn, carry):
-            where = {**at_shot(offset), **at_slab(turn)} if first_slab == 0 else at_slab(turn)
-            remote(mark_top, mark_top, sum_send.at[3], top_recv.at[0], where).start()
-            return carry
-
-        lax.fori_loop(first_slab, slabs, one, 0)
+    def tell(offset):
+        for turn in range(slabs):
+            if offset is not None or turn > 0:
+                where = {**({} if offset is None else at_shot(offset)), **at_slab(turn)}
+                remote(mark_top, mark_top, sum_send.at[3], top_recv.at[0], where).start()
 
     def share(piece):
         for offset in offsets:
@@ -355,10 +354,10 @@
             share(piece)
     tops[my_class * slabs + slab] = jnp.max(top, axis=0, keepdims=True)
     for number, offset in enumerate(offsets):
-        tell(offset, 0)
+        tell(offset)
         if number == 2:
             share(len(pieces) - 1)
-    tell(0, 1)
+    tell(None)
     for piece, (start, length, plane) in enumerate(pieces):
         absorb(part.at[:, slots(piece)], ag_recv.at[piece])
         for index in range(length):
@@ -440,10 +439,10 @@
                 pltpu.SemaphoreType.REGULAR((3,)),
                 pltpu.SemaphoreType.REGULAR((2,)),
                 dma((4,)),
-                dma((3,)),
-                dma((3, 2)),
-                dma((3, 2)),
-                dma((3,)),
+                dma((depth // 2,)),
+                dma((depth // 2, 2)),
+                dma((depth // 2, 2)),
+                dma((depth // 2,)),
                 dma((1,)),
             ],
             compiler_params=pltpu.CompilerParams(

time: 91.7 us -> 91 us (level)
  no operation moved by 1% of the time
where the time goes in v7:
time: 91 us; the launch traced here: 90.9 us
  Pallas kernels  89.6 us (98%)
  between operations  1.29 us (1%)
    pallas_call x1, Pallas kernels, per_device(): pl.pallas_call(functools.partial(kernel, shape, iters, shots, slabs), out...  88.7 us

profile of v7, /device:TPU:33, one launch (start us, length us, event | category | flops | bytes accessed | tf_op | source)
XLA Modules:
  0.0 90.9 jit_solution(6860325531781662023)
XLA Ops:
  1.3 88.7 %reverse_time.1 = (f32[8,64,128]{2,1,0:T(8,128)S(1)}, f32[1,128]{1,0:T(1,128)S(1)}, f32[8,64,128]{2,1,0:T(8,128)S(1)}, f32[8,64,128]{2,1,0:T(8,128)S(1)}, f32[8,...) custom-call(s32[1]{0:T(128)S(6)} %copy.12.src_index, f32[1,8]{1,0:T(1,128)} %wavelet_hbm.1, f32[1,8,128]{2,1,0:T(8,128)} %misfit_hbm.1, ...), custom_call_target="tpu_custom_call" | custom-call | tf_op jit(solution)/shard_map/reverse_time/pallas_call | solution.py:415
  90.0 0.9 %model_update.1 = (f32[8,64,128]{2,1,0:T(8,128)}, f32[1,8,64,128]{3,2,1,0:T(8,128)}, f32[1,8,64,128]{3,2,1,0:T(8,128)}) custom-call(f32[8,64,128]{2,1,0:T(8,128)S(1)} %get-tuple-element.9.grad, f32[1,128]{1,0:T(1,128)S(1)} %get-tuple-element.10.top, f32[8,64,128]{2,1,0:T(8,128)S(1)} %get-tuple-element.11.model, f32[8,64,128]{2,1,0:T(8,128)S(1)} %get-tuple-element.12.base, ...), custom_call_target="tpu_custom_call" | custom-call | tf_op jit(solution)/shard_map/model_update/pallas_call | solution.py:453

commit v8 on v7

--- a/solution.py
+++ b/solution.py
@@ -45,16 +45,26 @@
     def absorb(ref, sem):
         pltpu.make_async_copy(ref, ref, sem).wait()
 
-    loads = [
-        pltpu.make_async_copy(un_hbm.at[0], now.at[0, 0, own, body], load_sem.at[0]),
-        pltpu.make_async_copy(ul_hbm.at[0], mid.at[0, 0, own, body], load_sem.at[0]),
-        pltpu.make_async_copy(model_hbm, mod.at[own], load_sem.at[0]),
-        pltpu.make_async_copy(an_hbm.at[0], now.at[0, 1, own, body], load_sem.at[1]),
-        pltpu.make_async_copy(al_hbm.at[0], mid.at[0, 1, own, body], load_sem.at[1]),
-        pltpu.make_async_copy(misfit_hbm.at[0], misfit, load_sem.at[2]),
-        pltpu.make_async_copy(rec_hbm, rec, load_sem.at[3]),
-        pltpu.make_async_copy(wavelet_hbm, wavelet, load_sem.at[4]),
+    def load(source, target, width, near, rest):
+        spans = ((0, width, near), (depth - width, width, near), (width, depth - 2 * width, rest))
+        return [
+            pltpu.make_async_copy(source.at[pl.ds(start, size)], target(pl.ds(2 + start, size)), load_sem.at[sem])
+            for start, size, sem in spans
+        ]
+
+    groups = [
+        load(un_hbm.at[0], lambda planes: now.at[0, 0, planes, body], 2, 0, 2),
+        load(ul_hbm.at[0], lambda planes: mid.at[0, 0, planes, body], 1, 0, 2),
+        load(model_hbm, lambda planes: mod.at[planes], 1, 0, 2),
+        load(an_hbm.at[0], lambda planes: now.at[0, 1, planes, body], 2, 1, 3),
+        load(al_hbm.at[0], lambda planes: mid.at[0, 1, planes, body], 1, 1, 3),
     ]
+    small = [
+        pltpu.make_async_copy(misfit_hbm.at[0], misfit, load_sem.at[4]),
+        pltpu.make_async_copy(rec_hbm, rec, load_sem.at[5]),
+        pltpu.make_async_copy(wavelet_hbm, wavelet, load_sem.at[6]),
+    ]
+    loads = [copy for group in groups for copy in group[:2]] + small + [group[2] for group in groups]
     for copy in loads:
         copy.start()
     barrier = pltpu.get_barrier_semaphore()
@@ -108,9 +118,9 @@
     def last_u(side):
         send(side, now.at[rounds, 0, edge(side), body], now.at[rounds, 0, ghost(1 - side), body], rounds, 0)
 
-    absorb(inj.at[0:2, 0 : depth + 4], load_sem.at[0])
+    absorb(inj.at[0, 0:8], load_sem.at[0])
     on_sides(first_u)
-    absorb(inj.at[0:2, 0:depth], load_sem.at[1])
+    absorb(inj.at[0, 0:6], load_sem.at[1])
     on_sides(first_a)
     for offset in (1, -1):
         signal(far_sem.at[0], at_shot(offset))
@@ -141,7 +151,7 @@
                     for rnd in range(rounds + 1):
                         now[rnd, field, at, body, :] = plane0
 
-    for copy in loads[-3:]:
+    for copy in small:
         copy.wait()
     line = lax.shift_right_logical(rec[...], 7)
     lane = jnp.bitwise_and(rec[...], cols - 1)
@@ -178,6 +188,8 @@
 
     lax.fori_loop(0, 2, place, 0, unroll=True)
 
+    absorb(inj.at[0:2, 0:depth], load_sem.at[2])
+    absorb(inj.at[0:2, 0 : depth - 3], load_sem.at[3])
     first_lane = col_id == 0
     last_lane = col_id == cols - 1
 
@@ -433,7 +445,7 @@
                 pltpu.VMEM((shots // WINDOW, depth, height, cols), f32),
                 pltpu.VMEM(shape, f32),
                 pltpu.VMEM((WINDOW * slabs, 1, cols), f32),
-                dma((5,)),
+                dma((7,)),
                 dma((2,)),
                 dma((2, 2, 2)),
                 pltpu.SemaphoreType.REGULAR((3,)),

time: 91 us -> 91.1 us (level)
  no operation moved by 1% of the time
where the time goes in v8:
time: 91.1 us; the launch traced here: 90.9 us
  Pallas kernels  89.6 us (98%)
  between operations  1.29 us (1%)
    pallas_call x1, Pallas kernels, per_device(): pl.pallas_call(functools.partial(kernel, shape, iters, shots, slabs), out...  88.7 us

profile of v8, /device:TPU:33, one launch (start us, length us, event | category | flops | bytes accessed | tf_op | source)
XLA Modules:
  0.0 90.9 jit_solution(15531352683780995831)
XLA Ops:
  1.3 88.7 %reverse_time.1 = (f32[8,64,128]{2,1,0:T(8,128)S(1)}, f32[1,128]{1,0:T(1,128)S(1)}, f32[8,64,128]{2,1,0:T(8,128)S(1)}, f32[8,64,128]{2,1,0:T(8,128)S(1)}, f32[8,...) custom-call(s32[1]{0:T(128)S(6)} %copy.12.src_index, f32[1,8]{1,0:T(1,128)} %wavelet_hbm.1, f32[1,8,128]{2,1,0:T(8,128)} %misfit_hbm.1, ...), custom_call_target="tpu_custom_call" | custom-call | tf_op jit(solution)/shard_map/reverse_time/pallas_call | solution.py:427
  90.0 0.9 %model_update.1 = (f32[8,64,128]{2,1,0:T(8,128)}, f32[1,8,64,128]{3,2,1,0:T(8,128)}, f32[1,8,64,128]{3,2,1,0:T(8,128)}) custom-call(f32[8,64,128]{2,1,0:T(8,128)S(1)} %get-tuple-element.9.grad, f32[1,128]{1,0:T(1,128)S(1)} %get-tuple-element.10.top, f32[8,64,128]{2,1,0:T(8,128)S(1)} %get-tuple-element.11.model, f32[8,64,128]{2,1,0:T(8,128)S(1)} %get-tuple-element.12.base, ...), custom_call_target="tpu_custom_call" | custom-call | tf_op jit(solution)/shard_map/model_update/pallas_call | solution.py:465

commit v9 on v8

--- a/solution.py
+++ b/solution.py
@@ -367,7 +367,7 @@
     tops[my_class * slabs + slab] = jnp.max(top, axis=0, keepdims=True)
     for number, offset in enumerate(offsets):
         tell(offset)
-        if number == 2:
+        if number == 4:
             share(len(pieces) - 1)
     tell(None)
     for piece, (start, length, plane) in enumerate(pieces):

time: 91.1 us -> 91.1 us (level)
  no operation moved by 1% of the time
where the time goes in v9:
time: 91.1 us; the launch traced here: 90.9 us
  Pallas kernels  89.6 us (98%)
  between operations  1.29 us (1%)
    pallas_call x1, Pallas kernels, per_device(): pl.pallas_call(functools.partial(kernel, shape, iters, shots, slabs), out...  88.7 us

profile of v9, /device:TPU:33, one launch (start us, length us, event | category | flops | bytes accessed | tf_op | source)
XLA Modules:
  0.0 90.9 jit_solution(11855099379796185840)
XLA Ops:
  1.3 88.7 %reverse_time.1 = (f32[8,64,128]{2,1,0:T(8,128)S(1)}, f32[1,128]{1,0:T(1,128)S(1)}, f32[8,64,128]{2,1,0:T(8,128)S(1)}, f32[8,64,128]{2,1,0:T(8,128)S(1)}, f32[8,...) custom-call(s32[1]{0:T(128)S(6)} %copy.12.src_index, f32[1,8]{1,0:T(1,128)} %wavelet_hbm.1, f32[1,8,128]{2,1,0:T(8,128)} %misfit_hbm.1, ...), custom_call_target="tpu_custom_call" | custom-call | tf_op jit(solution)/shard_map/reverse_time/pallas_call | solution.py:427
  90.0 0.9 %model_update.1 = (f32[8,64,128]{2,1,0:T(8,128)}, f32[1,8,64,128]{3,2,1,0:T(8,128)}, f32[1,8,64,128]{3,2,1,0:T(8,128)}) custom-call(f32[8,64,128]{2,1,0:T(8,128)S(1)} %get-tuple-element.9.grad, f32[1,128]{1,0:T(1,128)S(1)} %get-tuple-element.10.top, f32[8,64,128]{2,1,0:T(8,128)S(1)} %get-tuple-element.11.model, f32[8,64,128]{2,1,0:T(8,128)S(1)} %get-tuple-element.12.base, ...), custom_call_target="tpu_custom_call" | custom-call | tf_op jit(solution)/shard_map/model_update/pallas_call | solution.py:465
